TPU v7x, 32 devices: a whole 2x2x4 slice. The times are simulated.
32 devices in a mesh: dp: 32 (over z, y, x, core).
Axes of the slice: x: 2, y: 2, z: 4, core: 2. Of those that a mesh axis runs over, the one named last changes fastest.
Arguments:
- g_mat: bfloat16 [32, 2457600], P('dp')
- g_vec: bfloat16 [32, 8320], P('dp')
- p_mat: float32 [2457600], P('dp')
- m_mat: float32 [2457600], P('dp')
- v_mat: float32 [2457600], P('dp')
- p_vec: float32 [8320], replicated
- m_vec: float32 [8320], replicated
- v_vec: float32 [8320], replicated
- learn_rate: float32 [], replicated
Outputs:
- output 1: float32 [2457600], P('dp')
- output 2: float32 [2457600], P('dp')
- output 3: float32 [2457600], P('dp')
- output 4: float32 [8320], replicated
- output 5: float32 [8320], replicated
- output 6: float32 [8320], replicated
- output 7: bfloat16 [2457600], replicated
All inputs are finite; a program needn't handle non-finite values.
Results may differ from a plain program's by a relative error of at most 0.001.
Values are sent between devices in bfloat16 or wider.
A program may use at most 1 GiB of HBM per device.

v0:
```python
import jax
import jax.numpy as jnp
from jax import lax
from jax.sharding import PartitionSpec as P

STEP = 10
ADAM_BETA1 = 0.9
ADAM_BETA2 = 0.98
ADAM_EPS = 1e-8
WEIGHT_DECAY = 0.01
MAX_NORM = 1.0
NORM_EPS = 1e-6
BIAS_ONE = 1.0 - ADAM_BETA1 ** STEP
BIAS_TWO = 1.0 - ADAM_BETA2 ** STEP


def adam_update(grad_vals, param_vals, moment_one, moment_two, learn_rate, decay_rate):
    new_one = ADAM_BETA1 * moment_one + (1.0 - ADAM_BETA1) * grad_vals
    new_two = ADAM_BETA2 * moment_two + (1.0 - ADAM_BETA2) * grad_vals * grad_vals
    direction = (new_one / BIAS_ONE) / (jnp.sqrt(new_two / BIAS_TWO) + ADAM_EPS)
    return param_vals - learn_rate * (direction + decay_rate * param_vals), new_one, new_two


def solution(mesh):
    axis_name = mesh.axis_names[0]
    group_size = mesh.shape[axis_name]

    def local_step(g_mat, g_vec, p_mat, m_mat, v_mat, p_vec, m_vec, v_vec, learn_rate):
        send_rows = g_mat.reshape(group_size, -1)
        recv_rows = lax.all_to_all(send_rows, axis_name, 0, 0, tiled=True)
        grad_mat = jnp.sum(recv_rows.astype(jnp.float32), axis=0) / group_size
        grad_vec = lax.psum(g_vec[0].astype(jnp.float32), axis_name) / group_size
        norm_sq = lax.psum(jnp.sum(grad_mat * grad_mat), axis_name) + jnp.sum(grad_vec * grad_vec)
        clip_scale = jnp.minimum(1.0, MAX_NORM / (jnp.sqrt(norm_sq) + NORM_EPS))
        new_p_mat, new_m_mat, new_v_mat = adam_update(grad_mat * clip_scale, p_mat, m_mat, v_mat, learn_rate, WEIGHT_DECAY)
        new_p_vec, new_m_vec, new_v_vec = adam_update(grad_vec * clip_scale, p_vec, m_vec, v_vec, learn_rate, 0.0)
        full_params = lax.all_gather(new_p_mat.astype(jnp.bfloat16), axis_name, tiled=True)
        return new_p_mat, new_m_mat, new_v_mat, new_p_vec, new_m_vec, new_v_vec, full_params

    return jax.shard_map(
        local_step,
        mesh=mesh,
        in_specs=(P(axis_name, None), P(axis_name, None), P(axis_name), P(axis_name), P(axis_name), P(), P(), P(), P()),
        out_specs=(P(axis_name), P(axis_name), P(axis_name), P(), P(), P(), P()),
        check_vma=False,
    )
```

profile of v0, /device:TPU:0, one launch (start us, length us, event | category | flops | bytes accessed | tf_op | source)
XLA Modules:
  0.0 386.2 jit_solution(10052531952921654487)
XLA Ops:
  7.2 0.5 broadcast.9
  7.7 102.3 %reduce.3 = bf16[32,76800]{1,0:T(8,128)(2,1)} reduce(bf16[32,1,76800]{2,1,0:T(2,128)(2,1)} %bitcast.1, bf16[]{:T(256)} %broadcast.9), dimensions={1}, to_apply=%bitcast.reduce_sub_computation | reduce | bytes 9830402 | tf_op jit(solution)/shard_map/all_to_all | solution.py:30
  110.0 7.3 %reshape.23 = bf16[32,2,38400]{2,1,0:T(2,128)(2,1)} reshape(bf16[32,76800]{1,0:T(8,128)(2,1)} %reduce.3) | data formatting | bytes 9830400
  117.3 0.0 copy-start.6
  117.3 7.5 %all-to-all-start = ((bf16[32,2,38400]{2,1,0:T(2,128)(2,1)}), bf16[32,2,38400]{2,1,0:T(2,128)(2,1)}, u32[]{:S(2)}, u32[]{:S(2)}) async-start(bf16[32,2,38400]{2,1,0:T(2,128)(2,1)} %reshape.23), calls=%async_computation | async-start | bytes 9830400 | tf_op jit(solution)/shard_map/all_to_all | solution.py:30
  124.7 0.0 all-gather.2.cloned.1.call-start
  124.8 0.0 copy-done.6
  124.8 0.1 convert_reduce_fusion.1
  124.9 105.4 %all-to-all-done = bf16[32,2,38400]{2,1,0:T(2,128)(2,1)} async-done(((bf16[32,2,38400]{2,1,0:T(2,128)(2,1)}), bf16[32,2,38400]{2,1,0:T(2,128)(2,1)}, u32[]{:S(2)}, u32[]{:S(2)}) %all-to-all-start) | async-done | bytes 4915232 | tf_op jit(solution)/shard_map/all_to_all | solution.py:30
  230.3 20.0 %reshape.24 = bf16[32,1,76800]{2,1,0:T(2,128)(2,1)} reshape(bf16[32,2,38400]{2,1,0:T(2,128)(2,1)} %all-to-all-done) | data formatting | bytes 9830400
  250.3 0.0 copy-start
  250.3 0.0 copy-start.1
  250.3 0.0 copy-start.2
  250.4 0.0 copy-start.3
  250.4 0.0 copy-start.4
  250.4 0.0 copy-start.5
  250.4 11.4 %convert_reduce_fusion = f32[76800]{0:T(1024)S(1)} fusion(bf16[32,1,76800]{2,1,0:T(2,128)(2,1)} %reshape.24), kind=kLoop, calls=%fused_computation | loop fusion | flops 4838400 | bytes 5222400 | tf_op jit(solution)/shard_map/reduce_sum | solution.py:31
  261.8 0.7 multiply_reduce_fusion
  263.1 42.4 %all-reduce = (f32[]{:T(128)}, f32[8320]{0:T(1024)S(1)}) all-reduce(f32[]{:T(128)} %multiply_reduce_fusion, f32[8320]{0:T(1024)S(1)} %convert_reduce_fusion.1), channel_id=1, replica_groups=mesh['dp'=32] {'dp'}, use_global_device_ids=true, to_apply=%region_2.0 | all-reduce | flops 8321 | bytes 66568 | tf_op jit(solution)/shard_map/psum | solution.py:33
  305.5 0.6 multiply_reduce_fusion.1
  307.5 0.0 copy-done
  307.5 0.0 copy-done.1
  307.5 0.0 copy-done.2
  307.5 1.2 fusion.2
  308.7 0.0 all-gather.2.cloned.1.call-update
  308.7 0.0 copy-done.3
  308.7 0.0 copy-done.4
  308.7 0.0 copy-done.5
  308.7 0.7 multiply_subtract_fusion.1
  309.4 64.4 %all-gather.2.cloned.1.call-done = bf16[2457600]{0:T(1024)(128)(2,1)} async-done(((bf16[76800]{0:T(1024)(128)(2,1)}), bf16[2457600]{0:T(1024)(128)(2,1)}) %all-gather.2.cloned.1.call-update) | async-done | bytes 4915216 | tf_op jit(solution)/shard_map/all_gather | solution.py:37
  373.9 5.5 %copy.18 = bf16[2457600]{0:T(1024)(128)(2,1)} copy(bf16[2457600]{0:T(1024)(128)(2,1)} %all-gather.2.cloned.1.call-done) | data formatting | bytes 9830400
Async XLA Ops:
  117.3 7.5 %copy-start.6 = (bf16[1,8320]{1,0:T(2,128)(2,1)S(1)}, bf16[1,8320]{1,0:T(2,128)(2,1)}, u32[]{:S(2)}) copy-start(bf16[1,8320]{1,0:T(2,128)(2,1)} %param.10) | copy-start | bytes 49924
  117.3 113.1 %all-to-all-start = ((bf16[32,2,38400]{2,1,0:T(2,128)(2,1)}), bf16[32,2,38400]{2,1,0:T(2,128)(2,1)}, u32[]{:S(2)}, u32[]{:S(2)}) async-start(bf16[32,2,38400]{2,1,0:T(2,128)(2,1)} %reshape.23), calls=%async_computation | async-start | bytes 9830400 | tf_op jit(solution)/shard_map/all_to_all | solution.py:30
  124.7 249.1 %all-gather.2.cloned.1.call-start = ((), (), s32[]{:S(2)}) async-start(), calls=%async_computation.1 | async-start | bytes 5068800 | tf_op jit(solution)/shard_map/all_gather | solution.py:37
  250.3 57.2 %copy-start = (f32[76800]{0:T(1024)S(1)}, f32[76800]{0:T(1024)}, u32[]{:S(2)}) copy-start(f32[76800]{0:T(1024)} %param.11) | copy-start | bytes 921604
  250.3 57.2 %copy-start.1 = (f32[76800]{0:T(1024)S(1)}, f32[76800]{0:T(1024)}, u32[]{:S(2)}) copy-start(f32[76800]{0:T(1024)} %param.12) | copy-start | bytes 921604
  250.3 57.2 %copy-start.2 = (f32[76800]{0:T(1024)S(1)}, f32[76800]{0:T(1024)}, u32[]{:S(2)}) copy-start(f32[76800]{0:T(1024)} %param.13) | copy-start | bytes 921604
  250.4 58.4 %copy-start.3 = (f32[8320]{0:T(1024)S(1)}, f32[8320]{0:T(1024)}, u32[]{:S(2)}) copy-start(f32[8320]{0:T(1024)} %param.14) | copy-start | bytes 99844
  250.4 58.4 %copy-start.4 = (f32[8320]{0:T(1024)S(1)}, f32[8320]{0:T(1024)}, u32[]{:S(2)}) copy-start(f32[8320]{0:T(1024)} %param.15) | copy-start | bytes 99844
  250.4 58.4 %copy-start.5 = (f32[8320]{0:T(1024)S(1)}, f32[8320]{0:T(1024)}, u32[]{:S(2)}) copy-start(f32[8320]{0:T(1024)} %param.16) | copy-start | bytes 99844
Sparse Core Ops, SparseCore 0:
  308.8 64.9 all-gather.1
where the time goes:
time: 387 us; the launch traced here: 386 us
  waiting for transfers between devices  170 us (44%)
  other arithmetic  117 us (30%)
  blocking collectives  42.4 us (11%)
  local copies, waits for them, and re-layouts  33.3 us (9%)
  between operations  16.2 us (4%)
  starting transfers between devices  7.51 us (2%)
    all_to_all x1, waiting for transfers between devices, local_step(): recv_rows = lax.all_to_all(send_rows, axis_name, 0, 0, tiled=True)  105 us
    all_to_all x1, other arithmetic, local_step(): recv_rows = lax.all_to_all(send_rows, axis_name, 0, 0, tiled=True)  102 us
    all_gather x1, waiting for transfers between devices, local_step(): lax.all_gather(new_p_mat.astype(jnp.bfloat16), axis_name, tiled=True)  64.4 us
    psum x1, blocking collectives, local_step(): lax.psum(jnp.sum(grad_mat * grad_mat), axis_name)  42.4 us
    unnamed x17, local copies, waits for them, and re-layouts  32.8 us
    reduce_sum x1, other arithmetic, local_step(): grad_mat = jnp.sum(recv_rows.astype(jnp.float32), axis=0) / group_size  11.4 us
  transfers between devices with their start and end apart: 2, of which 2 were waited for; matrix products, arithmetic and copies ran while one was open for 0% of the time, Pallas kernels for 0%

commit v1 on v0

v1 whole, which is shorter than its diff:
```python
import jax
import jax.numpy as jnp
from jax import lax
from jax.experimental import pallas as pl
from jax.experimental.pallas import tpu as pltpu
from jax.sharding import PartitionSpec as P

STEP = 10
ADAM_BETA1 = 0.9
ADAM_BETA2 = 0.98
ADAM_EPS = 1e-8
WEIGHT_DECAY = 0.01
MAX_NORM = 1.0
NORM_EPS = 1e-6
BIAS_ONE = 1.0 - ADAM_BETA1 ** STEP
BIAS_TWO = 1.0 - ADAM_BETA2 ** STEP

MESH = pl.DeviceIdType.MESH
F32 = jnp.float32
BF16 = jnp.bfloat16
LANES = 128
CHUNK = 120


def adam_update(grad_vals, param_vals, moment_one, moment_two, learn_rate, decay_rate):
    new_one = ADAM_BETA1 * moment_one + (1.0 - ADAM_BETA1) * grad_vals
    new_two = ADAM_BETA2 * moment_two + (1.0 - ADAM_BETA2) * grad_vals * grad_vals
    direction = (new_one / BIAS_ONE) / (jnp.sqrt(new_two / BIAS_TWO) + ADAM_EPS)
    return param_vals - learn_rate * (direction + decay_rate * param_vals), new_one, new_two


def step_kernel(group, rows, vrows, axis_name):
    inv_group = 1.0 / group

    def body(g_ref, gv_ref, p_ref, m_ref, v_ref, pv_ref, mv_ref, vv_ref, lr_ref,
             pb_out, p_out, m_out, v_out, pv_out, mv_out, vv_out,
             own, pair, send_a, recv_a, send_b, recv_b, send_z, recv_z, grad, norm_rows,
             p_in, m_in, v_in, gv_own, gv_pair, gv_x, gv_xr, gv_y, gv_yr, gv_z, gv_zr, gv_sum,
             pv_in, mv_in, vv_in,
             own_sem, pair_s, pair_r, a_s, a_r, b_s, b_r, z_s, z_r, load_sem,
             vc_s, vc_r, vx_s, vx_r, vy_s, vy_r, vz_s, vz_r, n_s, n_r,
             gz_s, gz_r, gb_s, gb_r, ga_s, ga_r, gc_s, gc_r):
        me = lax.axis_index(axis_name)
        core = me % 2
        x = (me // 2) % 2
        y = (me // 4) % 2
        z = me // 8
        str_a = 2 + 2 * core
        str_b = 4 - 2 * core
        a = x + core * (y - x)
        b = y + core * (x - y)
        dev_c = me + 1 - 2 * core
        dev_a = me + (1 - 2 * a) * str_a
        dev_b = me + (1 - 2 * b) * str_b
        dev_x = me + (1 - 2 * x) * 2
        dev_y = me + (1 - 2 * y) * 4
        high = z // 2
        order = [3 - 3 * high, 2 - high, 1 - z + 4 * high, z]

        def dev_z(zq):
            return me + (zq - z) * 8

        def piece(zq, flip_a, flip_b):
            aq = 1 - a if flip_a else a
            bq = 1 - b if flip_b else b
            return zq * 8 + aq * str_a + bq * str_b + core

        def partner_piece(zq, flip_a, flip_b):
            aq = 1 - b if flip_a else b
            bq = 1 - a if flip_b else a
            return zq * 8 + aq * str_b + bq * str_a + 1 - core

        def remote(src, dst, s_sem, r_sem, dev):
            return pltpu.make_async_remote_copy(
                src_ref=src, dst_ref=dst, send_sem=s_sem, recv_sem=r_sem, device_id=(dev,), device_id_type=MESH)

        flips = [(True, True), (True, False), (False, True), (False, False)]
        own_copies = []
        for j in range(4):
            for k, (fa, fb) in enumerate(flips):
                src = g_ref.at[pl.ds(piece(order[j], fa, fb) * rows, rows)]
                own_copies.append(pltpu.make_async_copy(src, own.at[j * 4 + k], own_sem.at[j * 4 + k]))
        for copy in own_copies[:4]:
            copy.start()
        loads = [pltpu.make_async_copy(s, d, load_sem.at[i]) for i, (s, d) in enumerate([
            (gv_ref, gv_own), (p_ref, p_in), (m_ref, m_in), (v_ref, v_in),
            (pv_ref, pv_in), (mv_ref, mv_in), (vv_ref, vv_in)])]

        barrier = pltpu.get_barrier_semaphore()
        for i in range(group):
            @pl.when(i != me)
            def _():
                pl.semaphore_signal(barrier, inc=1, device_id=(i,), device_id_type=MESH)
        pl.semaphore_wait(barrier, group - 1)

        pair_copies = []
        for j in range(4):
            for k, (fa, fb) in enumerate(flips):
                src = g_ref.at[pl.ds(partner_piece(order[j], fa, fb) * rows, rows)]
                pair_copies.append(remote(src, pair.at[j * 4 + k], pair_s.at[j * 4 + k], pair_r.at[j * 4 + k], dev_c))
        for i in range(16):
            pair_copies[i].start()
            if i >= 4:
                own_copies[i].start()
        vec_pair = remote(gv_ref, gv_pair, vc_s.at[0], vc_r.at[0], dev_c)
        vec_pair.start()
        for load in loads:
            load.start()

        def chunks(fn):
            @pl.loop(0, rows // CHUNK)
            def _(i):
                fn(pl.ds(pl.multiple_of(i * CHUNK, 8), CHUNK))

        def pair_sum(i, s):
            return own[i, s, 0, :].astype(F32) + pair[i, s, 0, :].astype(F32)

        a_copies = [remote(send_a.at[i], recv_a.at[i], a_s.at[i], a_r.at[i], dev_a) for i in range(8)]
        for i in range(8):
            slot = (i // 2) * 4 + i % 2
            own_copies[slot].wait()
            pair_copies[slot].wait_recv()

            def add_pair(s, i=i, slot=slot):
                send_a[i, s, :] = pair_sum(slot, s)

            chunks(add_pair)
            a_copies[i].start()

        loads[0].wait()
        vec_pair.wait_recv()
        gv_x[...] = gv_own[:, 0, :].astype(F32) + gv_pair[:, 0, :].astype(F32)
        vec_x = remote(gv_x, gv_xr, vx_s.at[0], vx_r.at[0], dev_x)
        vec_x.start()

        b_copies = [remote(send_b.at[j], recv_b.at[j], b_s.at[j], b_r.at[j], dev_b) for j in range(4)]
        z_copies = [remote(send_z.at[j], recv_z.at[z], z_s.at[j], z_r.at[z], dev_z(order[j])) for j in range(3)]

        def do_b(j):
            slot = j * 4 + 2
            own_copies[slot].wait()
            pair_copies[slot].wait_recv()
            a_copies[j * 2].wait_recv()

            def add_a(s):
                send_b[j, s, :] = pair_sum(slot, s) + recv_a[j * 2, s, :]

            chunks(add_a)
            b_copies[j].start()

        def do_z(j):
            slot = j * 4 + 3
            own_copies[slot].wait()
            pair_copies[slot].wait_recv()
            a_copies[j * 2 + 1].wait_recv()
            b_copies[j].wait_recv()

            def add_ab(s):
                send_z[j, s, :] = pair_sum(slot, s) + recv_a[j * 2 + 1, s, :] + recv_b[j, s, :]

            chunks(add_ab)
            if j < 3:
                z_copies[j].start()

        do_b(0)
        vec_x.wait_recv()
        gv_y[...] = gv_x[...] + gv_xr[...]
        vec_y = remote(gv_y, gv_yr, vy_s.at[0], vy_r.at[0], dev_y)
        vec_y.start()
        do_b(1)
        do_z(0)
        do_b(2)
        vec_y.wait_recv()
        gv_z[...] = gv_y[...] + gv_yr[...]
        vec_z = [remote(gv_z, gv_zr.at[z], vz_s.at[j], vz_r.at[z], dev_z(order[j])) for j in range(3)]
        for copy in vec_z:
            copy.start()
        gv_zr[z] = gv_z[...]
        do_z(1)
        do_b(3)
        do_z(2)
        do_z(3)

        for j in range(3):
            remote(gv_z, gv_zr.at[order[j]], vz_s.at[j], vz_r.at[order[j]], dev_z(order[j])).wait_recv()
        gv_sum[...] = (((gv_zr[0] + gv_zr[1]) + gv_zr[2]) + gv_zr[3]) * inv_group
        vec_sq = jnp.sum(gv_sum[...] * gv_sum[...])

        for j in range(3):
            remote(send_z.at[j], recv_z.at[order[j]], z_s.at[j], z_r.at[order[j]], dev_z(order[j])).wait_recv()

        def final_sum(i, acc):
            s = pl.ds(pl.multiple_of(i * CHUNK, 8), CHUNK)
            g = send_z[3, s, :]
            for j in range(3):
                g = g + recv_z[order[j], s, :]
            g = g * inv_group
            grad[s, :] = g
            return acc + jnp.sum((g * g).reshape(CHUNK // 8, 8, LANES), axis=0)

        sq = lax.fori_loop(0, rows // CHUNK, final_sum, jnp.zeros((8, LANES), F32))
        norm_rows[me] = jnp.sum(sq, axis=0, keepdims=True)

        for d in range(1, group):
            to = (me + d) % group
            remote(norm_rows.at[me], norm_rows.at[me], n_s.at[d], n_r.at[d], to).start()
        for load in loads[1:]:
            load.wait()
        for d in range(1, group):
            frm = (me - d + group) % group
            remote(norm_rows.at[frm], norm_rows.at[frm], n_s.at[d], n_r.at[d], frm).wait_recv()
        norm_sq = jnp.sum(norm_rows[...]) + vec_sq
        norm = jnp.sqrt(jnp.full((8, LANES), norm_sq, F32))
        scale = jnp.minimum(1.0, MAX_NORM / (norm + NORM_EPS))[0:1, :]
        lr = lr_ref[0]

        def adam(s):
            new_p, new_m, new_v = adam_update(grad[s, :] * scale, p_in[s, :], m_in[s, :], v_in[s, :], lr, WEIGHT_DECAY)
            p_out[s, :] = new_p
            m_out[s, :] = new_m
            v_out[s, :] = new_v
            p_in[s, :] = new_p

        chunks(adam)
        pb_out[me] = p_in[...].astype(BF16)

        def move(idx, s_sem, r_sem, dev):
            return remote(pb_out.at[idx], pb_out.at[idx], s_sem, r_sem, dev)

        near = [z, order[2], order[1], order[0]]
        z_sends = [move(me, gz_s.at[q], gz_r.at[z], dev_z(near[q])) for q in range(1, 4)]
        b_idx = [piece(near[q], False, False) for q in range(4)]
        a_idx = [piece(near[i // 2], False, i % 2 == 1) for i in range(8)]
        c_idx = a_idx + [piece(near[i // 2], True, i % 2 == 1) for i in range(8)]
        b_sends = [move(b_idx[q], gb_s.at[q], gb_r.at[q], dev_b) for q in range(4)]
        a_sends = [move(a_idx[i], ga_s.at[i], ga_r.at[i], dev_a) for i in range(8)]
        c_sends = [move(c_idx[i], gc_s.at[i], gc_r.at[i], dev_c) for i in range(16)]

        def wait_z(q):
            idx = piece(near[q], False, False)
            move(idx, gz_s.at[q], gz_r.at[near[q]], dev_z(near[q])).wait_recv()

        def wait_b(q):
            move(piece(near[q], False, True), gb_s.at[q], gb_r.at[q], dev_b).wait_recv()

        def wait_a(i):
            move(c_idx[8 + i], ga_s.at[i], ga_r.at[i], dev_a).wait_recv()

        def wait_c(i):
            idx = partner_piece(near[(i % 8) // 2], i >= 8, i % 2 == 1)
            move(idx, gc_s.at[i], gc_r.at[i], dev_c).wait_recv()

        for q in range(3):
            z_sends[q].start()
        b_sends[0].start()
        a_sends[0].start()
        c_sends[0].start()

        pv_new, mv_new, vv_new = adam_update(gv_sum[...] * scale, pv_in[...], mv_in[...], vv_in[...], lr, 0.0)
        pv_out[...] = pv_new
        mv_out[...] = mv_new
        vv_out[...] = vv_new

        for q in range(4):
            if q > 0:
                wait_z(q)
                b_sends[q].start()
                a_sends[2 * q].start()
                c_sends[2 * q].start()
                for i in (2 * q - 2, 2 * q - 1):
                    wait_a(i)
                    c_sends[8 + i].start()
            wait_b(q)
            a_sends[2 * q + 1].start()
            c_sends[2 * q + 1].start()
        for i in (6, 7):
            wait_a(i)
            c_sends[8 + i].start()
        for i in range(16):
            wait_c(i)

        for copy in pair_copies + [vec_pair] + a_copies + [vec_x, vec_y] + b_copies + z_copies + vec_z:
            copy.wait_send()
        for d in range(1, group):
            remote(norm_rows.at[me], norm_rows.at[me], n_s.at[d], n_r.at[d], (me + d) % group).wait_send()
        for copy in z_sends + b_sends + a_sends + c_sends:
            copy.wait_send()

    vmem = pl.BlockSpec(memory_space=pltpu.VMEM)
    hbm = pl.BlockSpec(memory_space=pl.ANY)
    sems = pltpu.SemaphoreType.DMA
    return pl.pallas_call(
        body,
        name="adam_step",
        out_shape=(
            jax.ShapeDtypeStruct((group, rows, LANES), BF16),
            *[jax.ShapeDtypeStruct((rows, LANES), F32)] * 3,
            *[jax.ShapeDtypeStruct((vrows, LANES), F32)] * 3,
        ),
        in_specs=[hbm] * 8 + [pl.BlockSpec(memory_space=pltpu.SMEM)],
        out_specs=(vmem,) * 7,
        scratch_shapes=[
            pltpu.VMEM((16, rows, 1, LANES), BF16),
            pltpu.VMEM((16, rows, 1, LANES), BF16),
            pltpu.VMEM((8, rows, LANES), F32),
            pltpu.VMEM((8, rows, LANES), F32),
            pltpu.VMEM((4, rows, LANES), F32),
            pltpu.VMEM((4, rows, LANES), F32),
            pltpu.VMEM((4, rows, LANES), F32),
            pltpu.VMEM((4, rows, LANES), F32),
            pltpu.VMEM((rows, LANES), F32),
            pltpu.VMEM((group, 1, LANES), F32),
            *[pltpu.VMEM((rows, LANES), F32)] * 3,
            *[pltpu.VMEM((vrows, 1, LANES), BF16)] * 2,
            *[pltpu.VMEM((vrows, LANES), F32)] * 5,
            pltpu.VMEM((4, vrows, LANES), F32),
            *[pltpu.VMEM((vrows, LANES), F32)] * 4,
            sems((16,)), sems((16,)), sems((16,)),
            sems((8,)), sems((8,)), sems((4,)), sems((4,)), sems((4,)), sems((4,)), sems((7,)),
            sems((1,)), sems((1,)), sems((1,)), sems((1,)), sems((1,)), sems((1,)), sems((4,)), sems((4,)),
            sems((group,)), sems((group,)),
            sems((4,)), sems((4,)), sems((4,)), sems((4,)), sems((8,)), sems((8,)), sems((16,)), sems((16,)),
        ],
        compiler_params=pltpu.CompilerParams(
            collective_id=0, has_side_effects=True, vmem_limit_bytes=56 * 1024 * 1024),
    )


def store_kernel(shapes):
    def body(*refs):
        n = len(shapes)
        ins, outs, sem = refs[:n], refs[n:2 * n], refs[2 * n]
        copies = [pltpu.make_async_copy(ins[i], outs[i], sem.at[i]) for i in range(n)]
        for copy in copies:
            copy.start()
        for copy in copies:
            copy.wait()

    return pl.pallas_call(
        body,
        name="store_results",
        out_shape=tuple(shapes),
        in_specs=[pl.BlockSpec(memory_space=pltpu.VMEM)] * len(shapes),
        out_specs=tuple([pl.BlockSpec(memory_space=pl.ANY)] * len(shapes)),
        scratch_shapes=[pltpu.SemaphoreType.DMA((len(shapes),))],
    )


def solution(mesh):
    axis_name = mesh.axis_names[0]
    group = mesh.shape[axis_name]

    def local_step(g_mat, g_vec, p_mat, m_mat, v_mat, p_vec, m_vec, v_vec, learn_rate):
        rows = p_mat.shape[0] // LANES
        vrows = p_vec.shape[0] // LANES
        results = step_kernel(group, rows, vrows, axis_name)(
            g_mat.reshape(group * rows, 1, LANES), g_vec.reshape(vrows, 1, LANES),
            *[t.reshape(rows, LANES) for t in (p_mat, m_mat, v_mat)],
            *[t.reshape(vrows, LANES) for t in (p_vec, m_vec, v_vec)],
            learn_rate.reshape(1))
        results = store_kernel([jax.ShapeDtypeStruct(r.shape, r.dtype) for r in results])(*results)
        full, new_p, new_m, new_v, new_pv, new_mv, new_vv = results
        return (*[t.reshape(-1) for t in (new_p, new_m, new_v, new_pv, new_mv, new_vv)], full.reshape(-1))

    return jax.shard_map(
        local_step,
        mesh=mesh,
        in_specs=(P(axis_name, None), P(axis_name, None), P(axis_name), P(axis_name), P(axis_name), P(), P(), P(), P()),
        out_specs=(P(axis_name), P(axis_name), P(axis_name), P(), P(), P(), P()),
        check_vma=False,
    )
```

time: 387 us -> 115 us (0.30)
  waiting for transfers between devices: 170 us -> 0 us
  other arithmetic: 117 us -> 0 us
  Pallas kernels: 0 us -> 114 us
  blocking collectives: 42.4 us -> 0 us
  local copies, waits for them, and re-layouts: 33.3 us -> 0 us
  between operations: 16.2 us -> 1.29 us
  starting transfers between devices: 7.51 us -> 0 us
    pallas_call x0 -> x2, Pallas kernels: none -> 114 us  [the longest x1 109 us: local_step(): step_kernel(group, rows, vrows, axis_name)]
    all_to_all x1 -> x0, waiting for transfers between devices: 105 us -> none  [local_step(): recv_rows = lax.all_to_all(send_rows, axis_name, 0, 0, tiled=True)]
    all_to_all x1 -> x0, other arithmetic: 102 us -> none  [local_step(): recv_rows = lax.all_to_all(send_rows, axis_name, 0, 0, tiled=True)]
    all_gather x1 -> x0, waiting for transfers between devices: 64.4 us -> none  [local_step(): lax.all_gather(new_p_mat.astype(jnp.bfloat16), axis_name, tiled=True)]
    psum x1 -> x0, blocking collectives: 42.4 us -> none  [local_step(): lax.psum(jnp.sum(grad_mat * grad_mat), axis_name)]
    unnamed x17 -> x0, local copies, waits for them, and re-layouts: 32.8 us -> none
    reduce_sum x3 -> x0, other arithmetic: 12.7 us -> none  [the longest x1 11.4 us: local_step(): grad_mat = jnp.sum(recv_rows.astype(jnp.float32), axis=0) / group_size]
    all_to_all x1 -> x0, starting transfers between devices: 7.47 us -> none  [local_step(): recv_rows = lax.all_to_all(send_rows, axis_name, 0, 0, tiled=True)]
  transfers between devices with their start and end apart: 2 -> 0, of which waited for: 2 -> 0; matrix products, arithmetic and copies ran while one was open for 0% -> 0% of each run, Pallas kernels for 0% -> 0%
where the time goes in v1:
time: 115 us
  Pallas kernels  114 us (99%)
  between operations  1.29 us (1%)
    pallas_call x1, Pallas kernels, local_step(): step_kernel(group, rows, vrows, axis_name)  109 us
    pallas_call x1, Pallas kernels, local_step(): store_kernel([jax.ShapeDtypeStruct(r.shape, r.dtype) for r in results])  5.22 us

profile of v1, /device:TPU:0, one launch (start us, length us, event | category | flops | bytes accessed | tf_op | source)
XLA Modules:
  0.0 115.3 jit_solution(17872607838925917879)
XLA Ops:
  1.3 108.8 %adam_step.1 = (bf16[32,600,128]{2,1,0:T(8,128)(2,1)}, f32[600,128]{1,0:T(8,128)}, f32[600,128]{1,0:T(8,128)}, f32[600,128]{1,0:T(8,128)}, f32[65,128]{1,0:T(8,1...) custom-call(bf16[19200,1,128]{2,1,0:T(2,128)(2,1)} %bitcast.17, bf16[65,1,128]{2,1,0:T(2,128)(2,1)} %bitcast.24, ...), custom_call_target="tpu_custom_call" | custom-call | tf_op jit(solution)/shard_map/adam_step/pallas_call | solution.py:356
  110.1 5.2 %store_results.1 = (bf16[32,600,128]{2,1,0:T(8,128)(2,1)}, f32[600,128]{1,0:T(8,128)}, f32[600,128]{1,0:T(8,128)}, f32[600,128]{1,0:T(8,128)}, f32[65,128]{1,0:T...) custom-call(bf16[32,600,128]{2,1,0:T(8,128)(2,1)} %get-tuple-element.21.refs_0_, f32[600,128]{1,0:T(8,128)} %get-tuple-element.22.refs_1_, ...), custom_call_target="tpu_custom_call" | custom-call | tf_op jit(solution)/shard_map/store_results/pallas_call | solution.py:361

commit v2 on v1

--- a/solution.py
+++ b/solution.py
@@ -31,14 +31,16 @@
 
 def step_kernel(group, rows, vrows, axis_name):
     inv_group = 1.0 / group
+    vstep = vrows // 16 * 8
+    vhalf = vrows - vstep
 
     def body(g_ref, gv_ref, p_ref, m_ref, v_ref, pv_ref, mv_ref, vv_ref, lr_ref,
              pb_out, p_out, m_out, v_out, pv_out, mv_out, vv_out,
              own, pair, send_a, recv_a, send_b, recv_b, send_z, recv_z, grad, norm_rows,
-             p_in, m_in, v_in, gv_own, gv_pair, gv_x, gv_xr, gv_y, gv_yr, gv_z, gv_zr, gv_sum,
+             p_in, m_in, v_in, gv_own, gv_pair, gv_plane, gv_line, gv_half, gv_other, gv_sum,
              pv_in, mv_in, vv_in,
              own_sem, pair_s, pair_r, a_s, a_r, b_s, b_r, z_s, z_r, load_sem,
-             vc_s, vc_r, vx_s, vx_r, vy_s, vy_r, vz_s, vz_r, n_s, n_r,
+             vc_s, vc_r, vp_s, vp_r, vz_s, vz_r, ve_s, ve_r, n_s, n_r,
              gz_s, gz_r, gb_s, gb_r, ga_s, ga_r, gc_s, gc_r):
         me = lax.axis_index(axis_name)
         core = me % 2
@@ -54,6 +56,7 @@
         dev_b = me + (1 - 2 * b) * str_b
         dev_x = me + (1 - 2 * x) * 2
         dev_y = me + (1 - 2 * y) * 4
+        spot = y * 2 + x
         high = z // 2
         order = [3 - 3 * high, 2 - high, 1 - z + 4 * high, z]
 
@@ -80,31 +83,33 @@
             for k, (fa, fb) in enumerate(flips):
                 src = g_ref.at[pl.ds(piece(order[j], fa, fb) * rows, rows)]
                 own_copies.append(pltpu.make_async_copy(src, own.at[j * 4 + k], own_sem.at[j * 4 + k]))
-        for copy in own_copies[:4]:
-            copy.start()
+        use_order = [j * 4 + k for ks in ((0, 1), (2, 3)) for j in range(4) for k in ks]
+        for i in use_order[:4]:
+            own_copies[i].start()
         loads = [pltpu.make_async_copy(s, d, load_sem.at[i]) for i, (s, d) in enumerate([
-            (gv_ref, gv_own), (p_ref, p_in), (m_ref, m_in), (v_ref, v_in),
+            (gv_ref.at[pl.ds(core * vstep, vhalf)], gv_own), (p_ref, p_in), (m_ref, m_in), (v_ref, v_in),
             (pv_ref, pv_in), (mv_ref, mv_in), (vv_ref, vv_in)])]
 
         barrier = pltpu.get_barrier_semaphore()
-        for i in range(group):
-            @pl.when(i != me)
-            def _():
-                pl.semaphore_signal(barrier, inc=1, device_id=(i,), device_id_type=MESH)
-        pl.semaphore_wait(barrier, group - 1)
+        plane = [dev_x, dev_y, dev_x + dev_y - me]
+        partners = [dev_c] + plane + [dev_z(order[j]) for j in range(3)]
+        for partner in partners:
+            pl.semaphore_signal(barrier, inc=1, device_id=(partner,), device_id_type=MESH)
+        pl.semaphore_wait(barrier, len(partners))
 
         pair_copies = []
         for j in range(4):
             for k, (fa, fb) in enumerate(flips):
                 src = g_ref.at[pl.ds(partner_piece(order[j], fa, fb) * rows, rows)]
                 pair_copies.append(remote(src, pair.at[j * 4 + k], pair_s.at[j * 4 + k], pair_r.at[j * 4 + k], dev_c))
-        for i in range(16):
+        vec_pair = remote(gv_ref.at[pl.ds((1 - core) * vstep, vhalf)], gv_pair, vc_s.at[0], vc_r.at[0], dev_c)
+        loads[0].start()
+        vec_pair.start()
+        for n, i in enumerate(use_order):
             pair_copies[i].start()
-            if i >= 4:
+            if n >= 4:
                 own_copies[i].start()
-        vec_pair = remote(gv_ref, gv_pair, vc_s.at[0], vc_r.at[0], dev_c)
-        vec_pair.start()
-        for load in loads:
+        for load in loads[1:]:
             load.start()
 
         def chunks(fn):
@@ -114,6 +119,14 @@
 
         def pair_sum(i, s):
             return own[i, s, 0, :].astype(F32) + pair[i, s, 0, :].astype(F32)
+
+        loads[0].wait()
+        vec_pair.wait_recv()
+        gv_plane[spot] = gv_own[:, 0, :].astype(F32) + gv_pair[:, 0, :].astype(F32)
+        vec_plane = [remote(gv_plane.at[spot], gv_plane.at[spot], vp_s.at[i], vp_r.at[i], dev)
+                     for i, dev in enumerate(plane)]
+        for copy in vec_plane:
+            copy.start()
 
         a_copies = [remote(send_a.at[i], recv_a.at[i], a_s.at[i], a_r.at[i], dev_a) for i in range(8)]
         for i in range(8):
@@ -127,11 +140,12 @@
             chunks(add_pair)
             a_copies[i].start()
 
-        loads[0].wait()
-        vec_pair.wait_recv()
-        gv_x[...] = gv_own[:, 0, :].astype(F32) + gv_pair[:, 0, :].astype(F32)
-        vec_x = remote(gv_x, gv_xr, vx_s.at[0], vx_r.at[0], dev_x)
-        vec_x.start()
+        for i, other in enumerate((spot + 1 - 2 * x, spot + 2 - 4 * y, 3 - spot)):
+            remote(gv_plane.at[other], gv_plane.at[other], vp_s.at[i], vp_r.at[i], plane[i]).wait_recv()
+        gv_line[z] = ((gv_plane[0] + gv_plane[1]) + gv_plane[2]) + gv_plane[3]
+        vec_line = [remote(gv_line.at[z], gv_line.at[z], vz_s.at[j], vz_r.at[z], dev_z(order[j])) for j in range(3)]
+        for copy in vec_line:
+            copy.start()
 
         b_copies = [remote(send_b.at[j], recv_b.at[j], b_s.at[j], b_r.at[j], dev_b) for j in range(4)]
         z_copies = [remote(send_z.at[j], recv_z.at[z], z_s.at[j], z_r.at[z], dev_z(order[j])) for j in range(3)]
@@ -163,28 +177,22 @@
                 z_copies[j].start()
 
         do_b(0)
-        vec_x.wait_recv()
-        gv_y[...] = gv_x[...] + gv_xr[...]
-        vec_y = remote(gv_y, gv_yr, vy_s.at[0], vy_r.at[0], dev_y)
-        vec_y.start()
+        for j in range(3):
+            remote(gv_line.at[order[j]], gv_line.at[order[j]], vz_s.at[j], vz_r.at[order[j]], dev_z(order[j])).wait_recv()
+        gv_half[...] = (((gv_line[0] + gv_line[1]) + gv_line[2]) + gv_line[3]) * inv_group
+        vec_end = remote(gv_half, gv_other, ve_s.at[0], ve_r.at[0], dev_c)
+        vec_end.start()
         do_b(1)
+        vec_end.wait_recv()
+        gv_sum[pl.ds(pl.multiple_of(core * vstep, 8), vhalf), :] = gv_half[...]
+        gv_sum[pl.ds(pl.multiple_of((1 - core) * vstep, 8), vhalf), :] = gv_other[...]
+        vec_sq = jnp.sum(gv_sum[...] * gv_sum[...])
         do_z(0)
         do_b(2)
-        vec_y.wait_recv()
-        gv_z[...] = gv_y[...] + gv_yr[...]
-        vec_z = [remote(gv_z, gv_zr.at[z], vz_s.at[j], vz_r.at[z], dev_z(order[j])) for j in range(3)]
-        for copy in vec_z:
-            copy.start()
-        gv_zr[z] = gv_z[...]
         do_z(1)
         do_b(3)
         do_z(2)
         do_z(3)
-
-        for j in range(3):
-            remote(gv_z, gv_zr.at[order[j]], vz_s.at[j], vz_r.at[order[j]], dev_z(order[j])).wait_recv()
-        gv_sum[...] = (((gv_zr[0] + gv_zr[1]) + gv_zr[2]) + gv_zr[3]) * inv_group
-        vec_sq = jnp.sum(gv_sum[...] * gv_sum[...])
 
         for j in range(3):
             remote(send_z.at[j], recv_z.at[order[j]], z_s.at[j], z_r.at[order[j]], dev_z(order[j])).wait_recv()
@@ -279,7 +287,7 @@
         for i in range(16):
             wait_c(i)
 
-        for copy in pair_copies + [vec_pair] + a_copies + [vec_x, vec_y] + b_copies + z_copies + vec_z:
+        for copy in pair_copies + [vec_pair, vec_end] + vec_plane + vec_line + a_copies + b_copies + z_copies:
             copy.wait_send()
         for d in range(1, group):
             remote(norm_rows.at[me], norm_rows.at[me], n_s.at[d], n_r.at[d], (me + d) % group).wait_send()
@@ -287,7 +295,7 @@
             copy.wait_send()
 
     vmem = pl.BlockSpec(memory_space=pltpu.VMEM)
-    hbm = pl.BlockSpec(memory_space=pl.ANY)
+    hbm = pl.BlockSpec(memory_space=pltpu.HBM)
     sems = pltpu.SemaphoreType.DMA
     return pl.pallas_call(
         body,
@@ -311,18 +319,18 @@
             pltpu.VMEM((rows, LANES), F32),
             pltpu.VMEM((group, 1, LANES), F32),
             *[pltpu.VMEM((rows, LANES), F32)] * 3,
-            *[pltpu.VMEM((vrows, 1, LANES), BF16)] * 2,
-            *[pltpu.VMEM((vrows, LANES), F32)] * 5,
-            pltpu.VMEM((4, vrows, LANES), F32),
+            *[pltpu.VMEM((vhalf, 1, LANES), BF16)] * 2,
+            *[pltpu.VMEM((4, vhalf, LANES), F32)] * 2,
+            *[pltpu.VMEM((vhalf, LANES), F32)] * 2,
             *[pltpu.VMEM((vrows, LANES), F32)] * 4,
             sems((16,)), sems((16,)), sems((16,)),
             sems((8,)), sems((8,)), sems((4,)), sems((4,)), sems((4,)), sems((4,)), sems((7,)),
-            sems((1,)), sems((1,)), sems((1,)), sems((1,)), sems((1,)), sems((1,)), sems((4,)), sems((4,)),
+            sems((1,)), sems((1,)), sems((3,)), sems((3,)), sems((4,)), sems((4,)), sems((1,)), sems((1,)),
             sems((group,)), sems((group,)),
             sems((4,)), sems((4,)), sems((4,)), sems((4,)), sems((8,)), sems((8,)), sems((16,)), sems((16,)),
         ],
         compiler_params=pltpu.CompilerParams(
-            collective_id=0, has_side_effects=True, vmem_limit_bytes=56 * 1024 * 1024),
+            collective_id=0, has_side_effects=True, vmem_limit_bytes=30 * 1024 * 1024),
     )
 
 
@@ -341,8 +349,9 @@
         name="store_results",
         out_shape=tuple(shapes),
         in_specs=[pl.BlockSpec(memory_space=pltpu.VMEM)] * len(shapes),
-        out_specs=tuple([pl.BlockSpec(memory_space=pl.ANY)] * len(shapes)),
+        out_specs=tuple([pl.BlockSpec(memory_space=pltpu.HBM)] * len(shapes)),
         scratch_shapes=[pltpu.SemaphoreType.DMA((len(shapes),))],
+        compiler_params=pltpu.CompilerParams(vmem_limit_bytes=16 * 1024 * 1024),
     )
 
 
@@ -353,11 +362,12 @@
     def local_step(g_mat, g_vec, p_mat, m_mat, v_mat, p_vec, m_vec, v_vec, learn_rate):
         rows = p_mat.shape[0] // LANES
         vrows = p_vec.shape[0] // LANES
-        results = step_kernel(group, rows, vrows, axis_name)(
+        operands = [
             g_mat.reshape(group * rows, 1, LANES), g_vec.reshape(vrows, 1, LANES),
             *[t.reshape(rows, LANES) for t in (p_mat, m_mat, v_mat)],
-            *[t.reshape(vrows, LANES) for t in (p_vec, m_vec, v_vec)],
-            learn_rate.reshape(1))
+            *[t.reshape(vrows, LANES) for t in (p_vec, m_vec, v_vec)]]
+        operands = [pltpu.with_memory_space_constraint(t, pltpu.HBM) for t in operands]
+        results = step_kernel(group, rows, vrows, axis_name)(*operands, learn_rate.reshape(1))
         results = store_kernel([jax.ShapeDtypeStruct(r.shape, r.dtype) for r in results])(*results)
         full, new_p, new_m, new_v, new_pv, new_mv, new_vv = results
         return (*[t.reshape(-1) for t in (new_p, new_m, new_v, new_pv, new_mv, new_vv)], full.reshape(-1))

time: 115 us -> 94.4 us (0.82)
  Pallas kernels: 114 us -> 93 us
    pallas_call x1, Pallas kernels: 109 us -> 90.4 us  [local_step(): step_kernel(group, rows, vrows, axis_name)(*operands, learn_rate.reshape(1))]
    pallas_call x1, Pallas kernels: 5.22 us -> 2.6 us  [local_step(): store_kernel([jax.ShapeDtypeStruct(r.shape, r.dtype) for r in results])]
where the time goes in v2:
time: 94.4 us; the launch traced here: 94.3 us
  Pallas kernels  93 us (99%)
  between operations  1.29 us (1%)
    pallas_call x1, Pallas kernels, local_step(): step_kernel(group, rows, vrows, axis_name)(*operands, learn_rate.reshape(1))  90.4 us
    pallas_call x1, Pallas kernels, local_step(): store_kernel([jax.ShapeDtypeStruct(r.shape, r.dtype) for r in results])  2.6 us

profile of v2, /device:TPU:0, one launch (start us, length us, event | category | flops | bytes accessed | tf_op | source)
XLA Modules:
  0.0 94.3 jit_solution(5508375374823554058)
XLA Ops:
  1.3 90.4 %adam_step.1 = (bf16[32,600,128]{2,1,0:T(8,128)(2,1)S(1)}, f32[600,128]{1,0:T(8,128)S(1)}, f32[600,128]{1,0:T(8,128)S(1)}, f32[600,128]{1,0:T(8,128)S(1)}, f32[6...) custom-call(bf16[19200,1,128]{2,1,0:T(2,128)(2,1)} %bitcast.17, bf16[65,1,128]{2,1,0:T(2,128)(2,1)} %bitcast.24, ...), custom_call_target="tpu_custom_call" | custom-call | tf_op jit(solution)/shard_map/adam_step/pallas_call | solution.py:370
  91.7 2.6 %store_results.1 = (bf16[32,600,128]{2,1,0:T(8,128)(2,1)}, f32[600,128]{1,0:T(8,128)}, f32[600,128]{1,0:T(8,128)}, f32[600,128]{1,0:T(8,128)}, f32[65,128]{1,0:T...) custom-call(bf16[32,600,128]{2,1,0:T(8,128)(2,1)S(1)} %get-tuple-element.21.refs_0_, ...), custom_call_target="tpu_custom_call" | custom-call | tf_op jit(solution)/shard_map/store_results/pallas_call | solution.py:371

commit v3 on v2

--- a/solution.py
+++ b/solution.py
@@ -33,12 +33,17 @@
     inv_group = 1.0 / group
     vstep = vrows // 16 * 8
     vhalf = vrows - vstep
+    cut = (rows // 2 + 15) // 16 * 16
+    halves = [pl.ds(0, cut), pl.ds(cut, rows - cut)]
+    steps = []
+    for lo, hi in ((0, cut), (cut, rows)):
+        mid = lo + ((hi - lo) // 2 + 15) // 16 * 16
+        steps.append([(lo, mid - lo), (mid, hi - mid)])
 
     def body(g_ref, gv_ref, p_ref, m_ref, v_ref, pv_ref, mv_ref, vv_ref, lr_ref,
              pb_out, p_out, m_out, v_out, pv_out, mv_out, vv_out,
              own, pair, send_a, recv_a, send_b, recv_b, send_z, recv_z, grad, norm_rows,
-             p_in, m_in, v_in, gv_own, gv_pair, gv_plane, gv_line, gv_half, gv_other, gv_sum,
-             pv_in, mv_in, vv_in,
+             state, gv_own, gv_pair, gv_plane, gv_line, gv_half, gv_other, gv_sum, vec_state,
              own_sem, pair_s, pair_r, a_s, a_r, b_s, b_r, z_s, z_r, load_sem,
              vc_s, vc_r, vp_s, vp_r, vz_s, vz_r, ve_s, ve_r, n_s, n_r,
              gz_s, gz_r, gb_s, gb_r, ga_s, ga_r, gc_s, gc_r):
@@ -86,9 +91,11 @@
         use_order = [j * 4 + k for ks in ((0, 1), (2, 3)) for j in range(4) for k in ks]
         for i in use_order[:4]:
             own_copies[i].start()
-        loads = [pltpu.make_async_copy(s, d, load_sem.at[i]) for i, (s, d) in enumerate([
-            (gv_ref.at[pl.ds(core * vstep, vhalf)], gv_own), (p_ref, p_in), (m_ref, m_in), (v_ref, v_in),
-            (pv_ref, pv_in), (mv_ref, mv_in), (vv_ref, vv_in)])]
+        vec_load = pltpu.make_async_copy(gv_ref.at[pl.ds(core * vstep, vhalf)], gv_own, load_sem.at[0])
+        vec_load.start()
+
+        def wait_all(ref, sem):
+            remote(ref, ref, sem, sem, dev_c).wait_recv()
 
         barrier = pltpu.get_barrier_semaphore()
         plane = [dev_x, dev_y, dev_x + dev_y - me]
@@ -101,16 +108,17 @@
         for j in range(4):
             for k, (fa, fb) in enumerate(flips):
                 src = g_ref.at[pl.ds(partner_piece(order[j], fa, fb) * rows, rows)]
-                pair_copies.append(remote(src, pair.at[j * 4 + k], pair_s.at[j * 4 + k], pair_r.at[j * 4 + k], dev_c))
-        vec_pair = remote(gv_ref.at[pl.ds((1 - core) * vstep, vhalf)], gv_pair, vc_s.at[0], vc_r.at[0], dev_c)
-        loads[0].start()
+                pair_copies.append(remote(src, pair.at[j * 4 + k], pair_s, pair_r.at[j * 4 + k], dev_c))
+        vec_pair = remote(gv_ref.at[pl.ds((1 - core) * vstep, vhalf)], gv_pair, vc_s, vc_r, dev_c)
         vec_pair.start()
         for n, i in enumerate(use_order):
             pair_copies[i].start()
             if n >= 4:
                 own_copies[i].start()
-        for load in loads[1:]:
-            load.start()
+        for i, ref in enumerate((p_ref, m_ref, v_ref)):
+            pltpu.make_async_copy(ref, state.at[i], load_sem.at[1]).start()
+        for i, ref in enumerate((pv_ref, mv_ref, vv_ref)):
+            pltpu.make_async_copy(ref, vec_state.at[i], load_sem.at[2]).start()
 
         def chunks(fn):
             @pl.loop(0, rows // CHUNK)
@@ -120,15 +128,14 @@
         def pair_sum(i, s):
             return own[i, s, 0, :].astype(F32) + pair[i, s, 0, :].astype(F32)
 
-        loads[0].wait()
+        vec_load.wait()
         vec_pair.wait_recv()
         gv_plane[spot] = gv_own[:, 0, :].astype(F32) + gv_pair[:, 0, :].astype(F32)
-        vec_plane = [remote(gv_plane.at[spot], gv_plane.at[spot], vp_s.at[i], vp_r.at[i], dev)
-                     for i, dev in enumerate(plane)]
+        vec_plane = [remote(gv_plane.at[spot], gv_plane.at[spot], vp_s, vp_r, dev) for dev in plane]
         for copy in vec_plane:
             copy.start()
 
-        a_copies = [remote(send_a.at[i], recv_a.at[i], a_s.at[i], a_r.at[i], dev_a) for i in range(8)]
+        a_copies = [remote(send_a.at[i], recv_a.at[i], a_s, a_r.at[i], dev_a) for i in range(8)]
         for i in range(8):
             slot = (i // 2) * 4 + i % 2
             own_copies[slot].wait()
@@ -140,15 +147,14 @@
             chunks(add_pair)
             a_copies[i].start()
 
-        for i, other in enumerate((spot + 1 - 2 * x, spot + 2 - 4 * y, 3 - spot)):
-            remote(gv_plane.at[other], gv_plane.at[other], vp_s.at[i], vp_r.at[i], plane[i]).wait_recv()
+        wait_all(gv_plane.at[pl.ds(0, 3)], vp_r)
         gv_line[z] = ((gv_plane[0] + gv_plane[1]) + gv_plane[2]) + gv_plane[3]
-        vec_line = [remote(gv_line.at[z], gv_line.at[z], vz_s.at[j], vz_r.at[z], dev_z(order[j])) for j in range(3)]
+        vec_line = [remote(gv_line.at[z], gv_line.at[z], vz_s, vz_r, dev_z(order[j])) for j in range(3)]
         for copy in vec_line:
             copy.start()
 
-        b_copies = [remote(send_b.at[j], recv_b.at[j], b_s.at[j], b_r.at[j], dev_b) for j in range(4)]
-        z_copies = [remote(send_z.at[j], recv_z.at[z], z_s.at[j], z_r.at[z], dev_z(order[j])) for j in range(3)]
+        b_copies = [remote(send_b.at[j], recv_b.at[j], b_s, b_r.at[j], dev_b) for j in range(4)]
+        z_copies = [remote(send_z.at[j], recv_z.at[z], z_s, z_r, dev_z(order[j])) for j in range(3)]
 
         def do_b(j):
             slot = j * 4 + 2
@@ -177,25 +183,20 @@
                 z_copies[j].start()
 
         do_b(0)
-        for j in range(3):
-            remote(gv_line.at[order[j]], gv_line.at[order[j]], vz_s.at[j], vz_r.at[order[j]], dev_z(order[j])).wait_recv()
+        wait_all(gv_line.at[pl.ds(0, 3)], vz_r)
         gv_half[...] = (((gv_line[0] + gv_line[1]) + gv_line[2]) + gv_line[3]) * inv_group
-        vec_end = remote(gv_half, gv_other, ve_s.at[0], ve_r.at[0], dev_c)
+        vec_end = remote(gv_half, gv_other, ve_s, ve_r, dev_c)
         vec_end.start()
-        do_b(1)
+        do_z(0)
         vec_end.wait_recv()
         gv_sum[pl.ds(pl.multiple_of(core * vstep, 8), vhalf), :] = gv_half[...]
         gv_sum[pl.ds(pl.multiple_of((1 - core) * vstep, 8), vhalf), :] = gv_other[...]
         vec_sq = jnp.sum(gv_sum[...] * gv_sum[...])
-        do_z(0)
-        do_b(2)
-        do_z(1)
-        do_b(3)
-        do_z(2)
-        do_z(3)
-
-        for j in range(3):
-            remote(send_z.at[j], recv_z.at[order[j]], z_s.at[j], z_r.at[order[j]], dev_z(order[j])).wait_recv()
+        for j in range(1, 4):
+            do_b(j)
+            do_z(j)
+
+        wait_all(recv_z.at[pl.ds(0, 3)], z_r)
 
         def final_sum(i, acc):
             s = pl.ds(pl.multiple_of(i * CHUNK, 8), CHUNK)
@@ -211,92 +212,151 @@
 
         for d in range(1, group):
             to = (me + d) % group
-            remote(norm_rows.at[me], norm_rows.at[me], n_s.at[d], n_r.at[d], to).start()
-        for load in loads[1:]:
-            load.wait()
-        for d in range(1, group):
-            frm = (me - d + group) % group
-            remote(norm_rows.at[frm], norm_rows.at[frm], n_s.at[d], n_r.at[d], frm).wait_recv()
+            remote(norm_rows.at[me], norm_rows.at[me], n_s, n_r, to).start()
+        wait_all(state, load_sem.at[1])
+        wait_all(vec_state, load_sem.at[2])
+        wait_all(norm_rows.at[pl.ds(0, group - 1)], n_r)
         norm_sq = jnp.sum(norm_rows[...]) + vec_sq
         norm = jnp.sqrt(jnp.full((8, LANES), norm_sq, F32))
         scale = jnp.minimum(1.0, MAX_NORM / (norm + NORM_EPS))[0:1, :]
         lr = lr_ref[0]
 
-        def adam(s):
-            new_p, new_m, new_v = adam_update(grad[s, :] * scale, p_in[s, :], m_in[s, :], v_in[s, :], lr, WEIGHT_DECAY)
+        def adam(start, size):
+            s = pl.ds(start, size)
+            new_p, new_m, new_v = adam_update(grad[s, :] * scale, state[0, s, :], state[1, s, :], state[2, s, :], lr, WEIGHT_DECAY)
             p_out[s, :] = new_p
             m_out[s, :] = new_m
             v_out[s, :] = new_v
-            p_in[s, :] = new_p
-
-        chunks(adam)
-        pb_out[me] = p_in[...].astype(BF16)
-
-        def move(idx, s_sem, r_sem, dev):
-            return remote(pb_out.at[idx], pb_out.at[idx], s_sem, r_sem, dev)
-
-        near = [z, order[2], order[1], order[0]]
-        z_sends = [move(me, gz_s.at[q], gz_r.at[z], dev_z(near[q])) for q in range(1, 4)]
-        b_idx = [piece(near[q], False, False) for q in range(4)]
-        a_idx = [piece(near[i // 2], False, i % 2 == 1) for i in range(8)]
-        c_idx = a_idx + [piece(near[i // 2], True, i % 2 == 1) for i in range(8)]
-        b_sends = [move(b_idx[q], gb_s.at[q], gb_r.at[q], dev_b) for q in range(4)]
-        a_sends = [move(a_idx[i], ga_s.at[i], ga_r.at[i], dev_a) for i in range(8)]
-        c_sends = [move(c_idx[i], gc_s.at[i], gc_r.at[i], dev_c) for i in range(16)]
-
-        def wait_z(q):
-            idx = piece(near[q], False, False)
-            move(idx, gz_s.at[q], gz_r.at[near[q]], dev_z(near[q])).wait_recv()
-
-        def wait_b(q):
-            move(piece(near[q], False, True), gb_s.at[q], gb_r.at[q], dev_b).wait_recv()
-
-        def wait_a(i):
-            move(c_idx[8 + i], ga_s.at[i], ga_r.at[i], dev_a).wait_recv()
-
-        def wait_c(i):
-            idx = partner_piece(near[(i % 8) // 2], i >= 8, i % 2 == 1)
-            move(idx, gc_s.at[i], gc_r.at[i], dev_c).wait_recv()
-
-        for q in range(3):
-            z_sends[q].start()
-        b_sends[0].start()
-        a_sends[0].start()
-        c_sends[0].start()
-
-        pv_new, mv_new, vv_new = adam_update(gv_sum[...] * scale, pv_in[...], mv_in[...], vv_in[...], lr, 0.0)
-        pv_out[...] = pv_new
-        mv_out[...] = mv_new
-        vv_out[...] = vv_new
-
-        for q in range(4):
-            if q > 0:
-                wait_z(q)
-                b_sends[q].start()
-                a_sends[2 * q].start()
-                c_sends[2 * q].start()
-                for i in (2 * q - 2, 2 * q - 1):
-                    wait_a(i)
-                    c_sends[8 + i].start()
-            wait_b(q)
-            a_sends[2 * q + 1].start()
-            c_sends[2 * q + 1].start()
-        for i in (6, 7):
-            wait_a(i)
-            c_sends[8 + i].start()
-        for i in range(16):
-            wait_c(i)
-
-        for copy in pair_copies + [vec_pair, vec_end] + vec_plane + vec_line + a_copies + b_copies + z_copies:
-            copy.wait_send()
-        for d in range(1, group):
-            remote(norm_rows.at[me], norm_rows.at[me], n_s.at[d], n_r.at[d], (me + d) % group).wait_send()
-        for copy in z_sends + b_sends + a_sends + c_sends:
-            copy.wait_send()
+            pb_out[me, s, :] = new_p.astype(BF16)
+
+        def plane_at(r):
+            return r + high * (3 - 2 * r)
+
+        def move(idx, h, s_sem, r_sem, dev):
+            ref = pb_out.at[idx, halves[h]]
+            return remote(ref, ref, s_sem, r_sem, dev)
+
+        def send_line(r, h, to):
+            zq = plane_at(r)
+            move(piece(zq, False, False), h, gz_s, gz_r.at[zq * 2 + h], dev_z(plane_at(to))).start()
+
+        def move_b(zq, flip, h):
+            return move(piece(zq, False, flip), h, gb_s, gb_r.at[zq * 2 + h], dev_b)
+
+        def move_a(zq, flip_a, fb, h):
+            i = (zq * 2 + fb) * 2 + h
+            return move(piece(zq, flip_a, fb == 1), h, ga_s, ga_r.at[i], dev_a)
+
+        def move_c(zq, fa, fb, h):
+            return move(piece(zq, fa == 1, fb == 1), h, gc_s, gc_r, dev_c)
+
+        def from_line(r, h, onward_to=None):
+            zq = plane_at(r)
+            move(piece(zq, False, False), h, gz_s, gz_r.at[zq * 2 + h], dev_z(zq)).wait_recv()
+            if onward_to is not None:
+                send_line(r, h, onward_to)
+            share(r, h)
+
+        def share(r, h):
+            zq = plane_at(r)
+            move_b(zq, False, h).start()
+            move_a(zq, False, 0, h).start()
+            move_c(zq, 0, 0, h).start()
+
+        def from_b(r, h):
+            zq = plane_at(r)
+            move_b(zq, True, h).wait_recv()
+            move_a(zq, False, 1, h).start()
+            move_c(zq, 0, 1, h).start()
+
+        def from_a(r, fb, h):
+            zq = plane_at(r)
+            move_a(zq, True, fb, h).wait_recv()
+            move_c(zq, 1, fb, h).start()
+
+        def finish(line_pieces):
+            wait_all(pb_out.at[pl.ds(0, group // 2)], gc_r)
+            wait_all(pb_out.at[pl.ds(0, line_pieces)], gz_s)
+
+        def update_vector():
+            pv_new, mv_new, vv_new = adam_update(gv_sum[...] * scale, vec_state[0], vec_state[1], vec_state[2], lr, 0.0)
+            pv_out[...] = pv_new
+            mv_out[...] = mv_new
+            vv_out[...] = vv_new
+
+        inner = z + high * (3 - 2 * z)
+
+        @pl.when(inner == 0)
+        def _():
+            for h in range(2):
+                for start, size in steps[h]:
+                    adam(start, size)
+                send_line(0, h, 1)
+                send_line(0, h, 2)
+                share(0, h)
+            update_vector()
+            for h in range(2):
+                from_line(1, h)
+                from_b(0, h)
+            for h in range(2):
+                from_a(0, 0, h)
+            for r in (1, 2):
+                for h in range(2):
+                    from_line(r + 1, h)
+                    from_b(r, h)
+                for h in range(2):
+                    from_a(r - 1, 1, h)
+                    from_a(r, 0, h)
+            for h in range(2):
+                from_b(3, h)
+                from_a(2, 1, h)
+                from_a(3, 0, h)
+            for h in range(2):
+                from_a(3, 1, h)
+            finish(2)
+
+        @pl.when(inner == 1)
+        def _():
+            for h in range(2):
+                for start, size in steps[h]:
+                    adam(start, size)
+                send_line(1, h, 2)
+                send_line(1, h, 0)
+                share(1, h)
+            update_vector()
+            for h in range(2):
+                from_line(2, h, 0)
+                from_line(0, h)
+                from_b(1, h)
+            for h in range(2):
+                from_a(1, 0, h)
+            for h in range(2):
+                from_line(3, h, 0)
+                from_b(2, h)
+                from_b(0, h)
+            for h in range(2):
+                from_a(1, 1, h)
+                from_a(2, 0, h)
+                from_a(0, 0, h)
+            for h in range(2):
+                from_b(3, h)
+                from_a(2, 1, h)
+                from_a(0, 1, h)
+                from_a(3, 0, h)
+            for h in range(2):
+                from_a(3, 1, h)
+            finish(4)
+
+        for ref, sem in ((pair, pair_s), (gv_pair, vc_s), (gv_plane.at[pl.ds(0, 3)], vp_s),
+                         (gv_line.at[pl.ds(0, 3)], vz_s), (gv_half, ve_s), (send_a, a_s), (send_b, b_s),
+                         (send_z.at[pl.ds(0, 3)], z_s), (norm_rows.at[pl.ds(0, group - 1)], n_s),
+                         (pb_out.at[pl.ds(0, 4)], gb_s), (pb_out.at[pl.ds(0, 8)], ga_s),
+                         (pb_out.at[pl.ds(0, group // 2)], gc_s)):
+            wait_all(ref, sem)
 
     vmem = pl.BlockSpec(memory_space=pltpu.VMEM)
     hbm = pl.BlockSpec(memory_space=pltpu.HBM)
-    sems = pltpu.SemaphoreType.DMA
+    sem = sems = pltpu.SemaphoreType.DMA
     return pl.pallas_call(
         body,
         name="adam_step",
@@ -318,16 +378,15 @@
             pltpu.VMEM((4, rows, LANES), F32),
             pltpu.VMEM((rows, LANES), F32),
             pltpu.VMEM((group, 1, LANES), F32),
-            *[pltpu.VMEM((rows, LANES), F32)] * 3,
+            pltpu.VMEM((3, rows, LANES), F32),
             *[pltpu.VMEM((vhalf, 1, LANES), BF16)] * 2,
             *[pltpu.VMEM((4, vhalf, LANES), F32)] * 2,
             *[pltpu.VMEM((vhalf, LANES), F32)] * 2,
-            *[pltpu.VMEM((vrows, LANES), F32)] * 4,
-            sems((16,)), sems((16,)), sems((16,)),
-            sems((8,)), sems((8,)), sems((4,)), sems((4,)), sems((4,)), sems((4,)), sems((7,)),
-            sems((1,)), sems((1,)), sems((3,)), sems((3,)), sems((4,)), sems((4,)), sems((1,)), sems((1,)),
-            sems((group,)), sems((group,)),
-            sems((4,)), sems((4,)), sems((4,)), sems((4,)), sems((8,)), sems((8,)), sems((16,)), sems((16,)),
+            pltpu.VMEM((vrows, LANES), F32),
+            pltpu.VMEM((3, vrows, LANES), F32),
+            sems((16,)), sem, sems((16,)), sem, sems((8,)), sem, sems((4,)), sem, sem, sems((3,)),
+            *[sem] * 8, sem, sem,
+            sem, sems((8,)), sem, sems((8,)), sem, sems((16,)), sem, sem,
         ],
         compiler_params=pltpu.CompilerParams(
             collective_id=0, has_side_effects=True, vmem_limit_bytes=30 * 1024 * 1024),

time: 94.4 us -> 83.1 us (0.88)
  Pallas kernels: 93 us -> 81.7 us
    pallas_call x1, Pallas kernels: 90.4 us -> 79.1 us  [local_step(): step_kernel(group, rows, vrows, axis_name)(*operands, learn_rate.reshape(1))]
where the time goes in v3:
time: 83.1 us; the launch traced here: 83 us
  Pallas kernels  81.7 us (98%)
  between operations  1.29 us (2%)
    pallas_call x1, Pallas kernels, local_step(): step_kernel(group, rows, vrows, axis_name)(*operands, learn_rate.reshape(1))  79.1 us
    pallas_call x1, Pallas kernels, local_step(): store_kernel([jax.ShapeDtypeStruct(r.shape, r.dtype) for r in results])  2.6 us

profile of v3, /device:TPU:0, one launch (start us, length us, event | category | flops | bytes accessed | tf_op | source)
XLA Modules:
  0.0 83.0 jit_solution(7294947093106170145)
XLA Ops:
  1.3 79.1 %adam_step.1 = (bf16[32,600,128]{2,1,0:T(8,128)(2,1)S(1)}, f32[600,128]{1,0:T(8,128)S(1)}, f32[600,128]{1,0:T(8,128)S(1)}, f32[600,128]{1,0:T(8,128)S(1)}, f32[6...) custom-call(bf16[19200,1,128]{2,1,0:T(2,128)(2,1)} %bitcast.17, bf16[65,1,128]{2,1,0:T(2,128)(2,1)} %bitcast.24, ...), custom_call_target="tpu_custom_call" | custom-call | tf_op jit(solution)/shard_map/adam_step/pallas_call | solution.py:429
  80.4 2.6 %store_results.1 = (bf16[32,600,128]{2,1,0:T(8,128)(2,1)}, f32[600,128]{1,0:T(8,128)}, f32[600,128]{1,0:T(8,128)}, f32[600,128]{1,0:T(8,128)}, f32[65,128]{1,0:T...) custom-call(bf16[32,600,128]{2,1,0:T(8,128)(2,1)S(1)} %get-tuple-element.21.refs_0_, ...), custom_call_target="tpu_custom_call" | custom-call | tf_op jit(solution)/shard_map/store_results/pallas_call | solution.py:430

commit v4 on v3

--- a/solution.py
+++ b/solution.py
@@ -33,6 +33,7 @@
     inv_group = 1.0 / group
     vstep = vrows // 16 * 8
     vhalf = vrows - vstep
+    last = rows * 3 // 5 // CHUNK * CHUNK
     cut = (rows // 2 + 15) // 16 * 16
     halves = [pl.ds(0, cut), pl.ds(cut, rows - cut)]
     steps = []
@@ -42,9 +43,9 @@
 
     def body(g_ref, gv_ref, p_ref, m_ref, v_ref, pv_ref, mv_ref, vv_ref, lr_ref,
              pb_out, p_out, m_out, v_out, pv_out, mv_out, vv_out,
-             own, pair, send_a, recv_a, send_b, recv_b, send_z, recv_z, grad, norm_rows,
+             own, pair, send_a, recv_a, send_b, recv_b, send_z, recv_z, mid, mid_recv, mid_b, mid_b_recv, grad, norm_rows,
              state, gv_own, gv_pair, gv_plane, gv_line, gv_half, gv_other, gv_sum, vec_state,
-             own_sem, pair_s, pair_r, a_s, a_r, b_s, b_r, z_s, z_r, load_sem,
+             own_sem, pair_s, pair_r, a_s, a_r, b_s, b_r, z_s, z_r, m_s, m_r, mb_s, mb_r, load_sem,
              vc_s, vc_r, vp_s, vp_r, vz_s, vz_r, ve_s, ve_r, n_s, n_r,
              gz_s, gz_r, gb_s, gb_r, ga_s, ga_r, gc_s, gc_r):
         me = lax.axis_index(axis_name)
@@ -65,6 +66,11 @@
         high = z // 2
         order = [3 - 3 * high, 2 - high, 1 - z + 4 * high, z]
 
+        place = z + high * (3 - 2 * z)
+
+        def plane_at(r):
+            return r + high * (3 - 2 * r)
+
         def dev_z(zq):
             return me + (zq - z) * 8
 
@@ -110,9 +116,10 @@
                 src = g_ref.at[pl.ds(partner_piece(order[j], fa, fb) * rows, rows)]
                 pair_copies.append(remote(src, pair.at[j * 4 + k], pair_s, pair_r.at[j * 4 + k], dev_c))
         vec_pair = remote(gv_ref.at[pl.ds((1 - core) * vstep, vhalf)], gv_pair, vc_s, vc_r, dev_c)
-        vec_pair.start()
         for n, i in enumerate(use_order):
             pair_copies[i].start()
+            if n == 1:
+                vec_pair.start()
             if n >= 4:
                 own_copies[i].start()
         for i, ref in enumerate((p_ref, m_ref, v_ref)):
@@ -120,13 +127,31 @@
         for i, ref in enumerate((pv_ref, mv_ref, vv_ref)):
             pltpu.make_async_copy(ref, vec_state.at[i], load_sem.at[2]).start()
 
-        def chunks(fn):
-            @pl.loop(0, rows // CHUNK)
+        def chunks(start, stop, fn):
+            @pl.loop(0, (stop - start) // CHUNK)
             def _(i):
-                fn(pl.ds(pl.multiple_of(i * CHUNK, 8), CHUNK))
+                fn(pl.ds(pl.multiple_of(start + i * CHUNK, 8), CHUNK), pl.ds(pl.multiple_of(i * CHUNK, 8), CHUNK))
 
         def pair_sum(i, s):
             return own[i, s, 0, :].astype(F32) + pair[i, s, 0, :].astype(F32)
+
+        def move_a_sum(i, first):
+            part = pl.ds(0, last) if first else pl.ds(last, rows - last)
+            return remote(send_a.at[i, part], recv_a.at[i, part], a_s, a_r.at[i * 2 + first], dev_a)
+
+        def do_a(i, first):
+            slot = (i // 2) * 4 + i % 2
+            if not first:
+                own_copies[slot].wait()
+                pair_copies[slot].wait_recv()
+
+            def add_pair(s, _):
+                send_a[i, s, :] = pair_sum(slot, s)
+
+            chunks(*((0, last) if first else (last, rows)), add_pair)
+            move_a_sum(i, first).start()
+
+        do_a(0, 0)
 
         vec_load.wait()
         vec_pair.wait_recv()
@@ -135,17 +160,10 @@
         for copy in vec_plane:
             copy.start()
 
-        a_copies = [remote(send_a.at[i], recv_a.at[i], a_s, a_r.at[i], dev_a) for i in range(8)]
-        for i in range(8):
-            slot = (i // 2) * 4 + i % 2
-            own_copies[slot].wait()
-            pair_copies[slot].wait_recv()
-
-            def add_pair(s, i=i, slot=slot):
-                send_a[i, s, :] = pair_sum(slot, s)
-
-            chunks(add_pair)
-            a_copies[i].start()
+        for i in range(1, 8):
+            do_a(i, 0)
+        for i in (0, 2, 1, 4, 3, 5, 6, 7):
+            do_a(i, 1)
 
         wait_all(gv_plane.at[pl.ds(0, 3)], vp_r)
         gv_line[z] = ((gv_plane[0] + gv_plane[1]) + gv_plane[2]) + gv_plane[3]
@@ -153,61 +171,134 @@
         for copy in vec_line:
             copy.start()
 
+        def move_mid(j, kind, slot, r):
+            at = slot * 2 + kind
+            return remote(mid.at[j, kind], mid_recv.at[slot, kind], m_s, m_r.at[at], dev_z(plane_at(r)))
+
+        def do_mid(j):
+            for kind in (1, 0):
+                slot = j * 4 + 3 - kind
+                i = j * 2 + 1 - kind
+                own_copies[slot].wait()
+                pair_copies[slot].wait_recv()
+                move_a_sum(i, 0).wait_recv()
+
+                def add_a(s, t, kind=kind, slot=slot, i=i):
+                    mid[j, kind, t, :] = pair_sum(slot, s) + recv_a[i, s, :]
+
+                chunks(last, rows, add_a)
+                if j < 3:
+                    @pl.when(place == 0)
+                    def _(kind=kind):
+                        move_mid(j, kind, (2, 3, 0)[j], 1).start()
+                if j == 2:
+                    @pl.when(place == 1)
+                    def _(kind=kind):
+                        move_mid(j, kind, 0, 0).start()
+
+        def merge_mid(j):
+            @pl.when(place == 1)
+            def _():
+                for kind in (1, 0):
+                    move_mid(j, kind, 2 + j, 0).wait_recv()
+
+                    def add_end(_, t, kind=kind):
+                        mid[j, kind, t, :] = mid[j, kind, t, :] + mid_recv[2 + j, kind, t, :]
+
+                    chunks(last, rows, add_end)
+                    move_mid(j, kind, 1, 3 - j).start()
+
+        def mid_total(kind, t):
+            return mid[3, kind, t, :] + mid_recv[0, kind, t, :] + mid_recv[1, kind, t, :]
+
+        def wait_mid(kind):
+            for slot in range(2):
+                move_mid(3, kind, slot, 2).wait_recv()
+
+        mid_b_copy = remote(mid_b, mid_b_recv, mb_s, mb_r, dev_b)
+
+        def mid_second():
+            wait_mid(1)
+
+            def add_mid(_, t):
+                mid_b[t, :] = mid_total(1, t)
+
+            chunks(last, rows, add_mid)
+            mid_b_copy.start()
+
         b_copies = [remote(send_b.at[j], recv_b.at[j], b_s, b_r.at[j], dev_b) for j in range(4)]
         z_copies = [remote(send_z.at[j], recv_z.at[z], z_s, z_r, dev_z(order[j])) for j in range(3)]
 
         def do_b(j):
-            slot = j * 4 + 2
-            own_copies[slot].wait()
-            pair_copies[slot].wait_recv()
-            a_copies[j * 2].wait_recv()
-
-            def add_a(s):
-                send_b[j, s, :] = pair_sum(slot, s) + recv_a[j * 2, s, :]
-
-            chunks(add_a)
+            move_a_sum(j * 2, 1).wait_recv()
+
+            def add_a(s, _):
+                send_b[j, s, :] = pair_sum(j * 4 + 2, s) + recv_a[j * 2, s, :]
+
+            chunks(0, last, add_a)
             b_copies[j].start()
 
+        def plane_total(j, s):
+            return pair_sum(j * 4 + 3, s) + recv_a[j * 2 + 1, s, :] + recv_b[j, s, :]
+
         def do_z(j):
-            slot = j * 4 + 3
-            own_copies[slot].wait()
-            pair_copies[slot].wait_recv()
-            a_copies[j * 2 + 1].wait_recv()
+            move_a_sum(j * 2 + 1, 1).wait_recv()
             b_copies[j].wait_recv()
 
-            def add_ab(s):
-                send_z[j, s, :] = pair_sum(slot, s) + recv_a[j * 2 + 1, s, :] + recv_b[j, s, :]
-
-            chunks(add_ab)
+            def add_ab(s, _):
+                send_z[j, s, :] = plane_total(j, s)
+
             if j < 3:
+                chunks(0, last, add_ab)
                 z_copies[j].start()
 
-        do_b(0)
+        do_mid(0)
+        do_mid(1)
         wait_all(gv_line.at[pl.ds(0, 3)], vz_r)
         gv_half[...] = (((gv_line[0] + gv_line[1]) + gv_line[2]) + gv_line[3]) * inv_group
         vec_end = remote(gv_half, gv_other, ve_s, ve_r, dev_c)
         vec_end.start()
-        do_z(0)
+        do_mid(2)
+        merge_mid(0)
+        do_mid(3)
         vec_end.wait_recv()
         gv_sum[pl.ds(pl.multiple_of(core * vstep, 8), vhalf), :] = gv_half[...]
         gv_sum[pl.ds(pl.multiple_of((1 - core) * vstep, 8), vhalf), :] = gv_other[...]
         vec_sq = jnp.sum(gv_sum[...] * gv_sum[...])
-        for j in range(1, 4):
-            do_b(j)
-            do_z(j)
-
-        wait_all(recv_z.at[pl.ds(0, 3)], z_r)
-
-        def final_sum(i, acc):
+        do_b(0)
+        merge_mid(1)
+        do_b(1)
+        do_z(0)
+        do_b(2)
+        do_z(1)
+        do_z(2)
+        do_b(3)
+        mid_second()
+        wait_mid(0)
+        mid_b_copy.wait_recv()
+
+        def squares(acc, g):
+            return acc + jnp.sum((g * g).reshape(CHUNK // 8, 8, LANES), axis=0)
+
+        def final_mid(i, acc):
+            t = pl.ds(pl.multiple_of(i * CHUNK, 8), CHUNK)
+            g = (mid_total(0, t) + mid_b_recv[t, :]) * inv_group
+            grad[pl.ds(pl.multiple_of(last + i * CHUNK, 8), CHUNK), :] = g
+            return squares(acc, g)
+
+        def final_last(i, acc):
             s = pl.ds(pl.multiple_of(i * CHUNK, 8), CHUNK)
-            g = send_z[3, s, :]
+            g = plane_total(3, s)
             for j in range(3):
                 g = g + recv_z[order[j], s, :]
             g = g * inv_group
             grad[s, :] = g
-            return acc + jnp.sum((g * g).reshape(CHUNK // 8, 8, LANES), axis=0)
-
-        sq = lax.fori_loop(0, rows // CHUNK, final_sum, jnp.zeros((8, LANES), F32))
+            return squares(acc, g)
+
+        sq = lax.fori_loop(0, (rows - last) // CHUNK, final_mid, jnp.zeros((8, LANES), F32))
+        do_z(3)
+        wait_all(recv_z.at[pl.ds(0, 3)], z_r)
+        sq = lax.fori_loop(0, last // CHUNK, final_last, sq)
         norm_rows[me] = jnp.sum(sq, axis=0, keepdims=True)
 
         for d in range(1, group):
@@ -229,9 +320,6 @@
             v_out[s, :] = new_v
             pb_out[me, s, :] = new_p.astype(BF16)
 
-        def plane_at(r):
-            return r + high * (3 - 2 * r)
-
         def move(idx, h, s_sem, r_sem, dev):
             ref = pb_out.at[idx, halves[h]]
             return remote(ref, ref, s_sem, r_sem, dev)
@@ -284,9 +372,7 @@
             mv_out[...] = mv_new
             vv_out[...] = vv_new
 
-        inner = z + high * (3 - 2 * z)
-
-        @pl.when(inner == 0)
+        @pl.when(place == 0)
         def _():
             for h in range(2):
                 for start, size in steps[h]:
@@ -315,7 +401,7 @@
                 from_a(3, 1, h)
             finish(2)
 
-        @pl.when(inner == 1)
+        @pl.when(place == 1)
         def _():
             for h in range(2):
                 for start, size in steps[h]:
@@ -349,7 +435,7 @@
 
         for ref, sem in ((pair, pair_s), (gv_pair, vc_s), (gv_plane.at[pl.ds(0, 3)], vp_s),
                          (gv_line.at[pl.ds(0, 3)], vz_s), (gv_half, ve_s), (send_a, a_s), (send_b, b_s),
-                         (send_z.at[pl.ds(0, 3)], z_s), (norm_rows.at[pl.ds(0, group - 1)], n_s),
+                         (send_z.at[pl.ds(0, 3)], z_s), (mid.at[pl.ds(0, 3)], m_s), (mid_b, mb_s), (norm_rows.at[pl.ds(0, group - 1)], n_s),
                          (pb_out.at[pl.ds(0, 4)], gb_s), (pb_out.at[pl.ds(0, 8)], ga_s),
                          (pb_out.at[pl.ds(0, group // 2)], gc_s)):
             wait_all(ref, sem)
@@ -370,12 +456,10 @@
         scratch_shapes=[
             pltpu.VMEM((16, rows, 1, LANES), BF16),
             pltpu.VMEM((16, rows, 1, LANES), BF16),
-            pltpu.VMEM((8, rows, LANES), F32),
-            pltpu.VMEM((8, rows, LANES), F32),
-            pltpu.VMEM((4, rows, LANES), F32),
-            pltpu.VMEM((4, rows, LANES), F32),
-            pltpu.VMEM((4, rows, LANES), F32),
-            pltpu.VMEM((4, rows, LANES), F32),
+            *[pltpu.VMEM((8, rows, LANES), F32)] * 2,
+            *[pltpu.VMEM((4, last, LANES), F32)] * 4,
+            *[pltpu.VMEM((4, 2, rows - last, LANES), F32)] * 2,
+            *[pltpu.VMEM((rows - last, LANES), F32)] * 2,
             pltpu.VMEM((rows, LANES), F32),
             pltpu.VMEM((group, 1, LANES), F32),
             pltpu.VMEM((3, rows, LANES), F32),
@@ -384,12 +468,12 @@
             *[pltpu.VMEM((vhalf, LANES), F32)] * 2,
             pltpu.VMEM((vrows, LANES), F32),
             pltpu.VMEM((3, vrows, LANES), F32),
-            sems((16,)), sem, sems((16,)), sem, sems((8,)), sem, sems((4,)), sem, sem, sems((3,)),
+            sems((16,)), sem, sems((16,)), sem, sems((16,)), sem, sems((4,)), sem, sem, sem, sems((8,)), sem, sem, sems((3,)),
             *[sem] * 8, sem, sem,
             sem, sems((8,)), sem, sems((8,)), sem, sems((16,)), sem, sem,
         ],
         compiler_params=pltpu.CompilerParams(
-            collective_id=0, has_side_effects=True, vmem_limit_bytes=30 * 1024 * 1024),
+            collective_id=0, has_side_effects=True, vmem_limit_bytes=32 * 1024 * 1024),
     )
 
 

time: 83.1 us -> 80 us (0.963)
  Pallas kernels: 81.7 us -> 78.5 us
    pallas_call x1, Pallas kernels: 79.1 us -> 75.9 us  [local_step(): step_kernel(group, rows, vrows, axis_name)(*operands, learn_rate.reshape(1))]
where the time goes in v4:
time: 80 us; the launch traced here: 79.8 us
  Pallas kernels  78.5 us (98%)
  between operations  1.29 us (2%)
    pallas_call x1, Pallas kernels, local_step(): step_kernel(group, rows, vrows, axis_name)(*operands, learn_rate.reshape(1))  75.9 us
    pallas_call x1, Pallas kernels, local_step(): store_kernel([jax.ShapeDtypeStruct(r.shape, r.dtype) for r in results])  2.6 us

profile of v4, /device:TPU:0, one launch (start us, length us, event | category | flops | bytes accessed | tf_op | source)
XLA Modules:
  0.0 79.8 jit_solution(5646526068634563695)
XLA Ops:
  1.3 75.9 %adam_step.1 = (bf16[32,600,128]{2,1,0:T(8,128)(2,1)S(1)}, f32[600,128]{1,0:T(8,128)S(1)}, f32[600,128]{1,0:T(8,128)S(1)}, f32[600,128]{1,0:T(8,128)S(1)}, f32[6...) custom-call(bf16[19200,1,128]{2,1,0:T(2,128)(2,1)} %bitcast.17, bf16[65,1,128]{2,1,0:T(2,128)(2,1)} %bitcast.24, ...), custom_call_target="tpu_custom_call" | custom-call | tf_op jit(solution)/shard_map/adam_step/pallas_call | solution.py:513
  77.2 2.6 %store_results.1 = (bf16[32,600,128]{2,1,0:T(8,128)(2,1)}, f32[600,128]{1,0:T(8,128)}, f32[600,128]{1,0:T(8,128)}, f32[600,128]{1,0:T(8,128)}, f32[65,128]{1,0:T...) custom-call(bf16[32,600,128]{2,1,0:T(8,128)(2,1)S(1)} %get-tuple-element.21.refs_0_, ...), custom_call_target="tpu_custom_call" | custom-call | tf_op jit(solution)/shard_map/store_results/pallas_call | solution.py:514

commit v5 on v4

--- a/solution.py
+++ b/solution.py
@@ -19,7 +19,19 @@
 F32 = jnp.float32
 BF16 = jnp.bfloat16
 LANES = 128
-CHUNK = 120
+STEPS = 3
+
+
+END_PLAN = [
+    "z100", "b00", "z110", "b01", "b02", "z120", "a00", "z200", "b10", "z210", "b11", "z220",
+    "z121", "a01", "a10", "z300", "b20", "z310", "b21", "z320", "z221", "a11", "a20", "z321",
+    "b30", "b31", "a21", "a30", "a31",
+]
+INNER_PLAN = [
+    "z200", "z000", "b10", "z210", "z010", "b11", "b12", "z220", "z020", "a10", "z300", "b20",
+    "b00", "z310", "b21", "b01", "z320", "z221", "z021", "a11", "a20", "a00", "z321", "b30",
+    "b31", "a21", "a01", "a30", "a31",
+]
 
 
 def adam_update(grad_vals, param_vals, moment_one, moment_two, learn_rate, decay_rate):
@@ -33,21 +45,22 @@
     inv_group = 1.0 / group
     vstep = vrows // 16 * 8
     vhalf = vrows - vstep
-    last = rows * 3 // 5 // CHUNK * CHUNK
-    cut = (rows // 2 + 15) // 16 * 16
-    halves = [pl.ds(0, cut), pl.ds(cut, rows - cut)]
+    last = rows * 3 // 5 // (8 * STEPS) * (8 * STEPS)
+    early, late = 176, 352
+    bounds = (0, early, late, rows)
+    parts = [pl.ds(lo, hi - lo) for lo, hi in zip(bounds, bounds[1:])]
     steps = []
-    for lo, hi in ((0, cut), (cut, rows)):
-        mid = lo + ((hi - lo) // 2 + 15) // 16 * 16
-        steps.append([(lo, mid - lo), (mid, hi - mid)])
+    for lo, hi in zip(bounds, bounds[1:]):
+        half = lo + ((hi - lo) // 2 + 15) // 16 * 16
+        steps.append([(lo, half - lo), (half, hi - half)])
 
     def body(g_ref, gv_ref, p_ref, m_ref, v_ref, pv_ref, mv_ref, vv_ref, lr_ref,
              pb_out, p_out, m_out, v_out, pv_out, mv_out, vv_out,
              own, pair, send_a, recv_a, send_b, recv_b, send_z, recv_z, mid, mid_recv, mid_b, mid_b_recv, grad, norm_rows,
              state, gv_own, gv_pair, gv_plane, gv_line, gv_half, gv_other, gv_sum, vec_state,
-             own_sem, pair_s, pair_r, a_s, a_r, b_s, b_r, z_s, z_r, m_s, m_r, mb_s, mb_r, load_sem,
+             own_sem, pool, pair_s, a_s, b_s, z_s, z_r, m_s, mb_s, mb_r, load_sem,
              vc_s, vc_r, vp_s, vp_r, vz_s, vz_r, ve_s, ve_r, n_s, n_r,
-             gz_s, gz_r, gb_s, gb_r, ga_s, ga_r, gc_s, gc_r):
+             gz_s, gb_s, ga_s, gc_s, gc_r):
         me = lax.axis_index(axis_name)
         core = me % 2
         x = (me // 2) % 2
@@ -93,7 +106,8 @@
         for j in range(4):
             for k, (fa, fb) in enumerate(flips):
                 src = g_ref.at[pl.ds(piece(order[j], fa, fb) * rows, rows)]
-                own_copies.append(pltpu.make_async_copy(src, own.at[j * 4 + k], own_sem.at[j * 4 + k]))
+                group_of = 0 if j + k == 0 else 1 + k // 2
+                own_copies.append(pltpu.make_async_copy(src, own.at[j * 4 + k], own_sem.at[group_of]))
         use_order = [j * 4 + k for ks in ((0, 1), (2, 3)) for j in range(4) for k in ks]
         for i in use_order[:4]:
             own_copies[i].start()
@@ -114,7 +128,8 @@
         for j in range(4):
             for k, (fa, fb) in enumerate(flips):
                 src = g_ref.at[pl.ds(partner_piece(order[j], fa, fb) * rows, rows)]
-                pair_copies.append(remote(src, pair.at[j * 4 + k], pair_s, pair_r.at[j * 4 + k], dev_c))
+                arrival = pool.at[j * 2 + k if k < 2 else 8 + j // 2]
+                pair_copies.append(remote(src, pair.at[j * 4 + k], pair_s, arrival, dev_c))
         vec_pair = remote(gv_ref.at[pl.ds((1 - core) * vstep, vhalf)], gv_pair, vc_s, vc_r, dev_c)
         for n, i in enumerate(use_order):
             pair_copies[i].start()
@@ -128,21 +143,29 @@
             pltpu.make_async_copy(ref, vec_state.at[i], load_sem.at[2]).start()
 
         def chunks(start, stop, fn):
-            @pl.loop(0, (stop - start) // CHUNK)
+            size = (stop - start) // STEPS
+
+            @pl.loop(0, STEPS)
             def _(i):
-                fn(pl.ds(pl.multiple_of(start + i * CHUNK, 8), CHUNK), pl.ds(pl.multiple_of(i * CHUNK, 8), CHUNK))
+                fn(pl.ds(pl.multiple_of(start + i * size, 8), size), pl.ds(pl.multiple_of(i * size, 8), size))
 
         def pair_sum(i, s):
             return own[i, s, 0, :].astype(F32) + pair[i, s, 0, :].astype(F32)
 
         def move_a_sum(i, first):
             part = pl.ds(0, last) if first else pl.ds(last, rows - last)
-            return remote(send_a.at[i, part], recv_a.at[i, part], a_s, a_r.at[i * 2 + first], dev_a)
+            return remote(send_a.at[i, part], recv_a.at[i, part], a_s, pool.at[10 + i * 2 + first], dev_a)
+
+        loaded = set()
 
         def do_a(i, first):
             slot = (i // 2) * 4 + i % 2
-            if not first:
-                own_copies[slot].wait()
+            if slot not in loaded:
+                loaded.add(slot)
+                if len(loaded) == 1:
+                    own_copies[0].wait()
+                if len(loaded) == 2:
+                    wait_all(own.at[pl.ds(0, 7)], own_sem.at[1])
                 pair_copies[slot].wait_recv()
 
             def add_pair(s, _):
@@ -160,10 +183,8 @@
         for copy in vec_plane:
             copy.start()
 
-        for i in range(1, 8):
-            do_a(i, 0)
-        for i in (0, 2, 1, 4, 3, 5, 6, 7):
-            do_a(i, 1)
+        for i, first in [(1, 0), (2, 0), (3, 0), (4, 0), (5, 0), (0, 1), (2, 1), (6, 0), (7, 0), (1, 1), (4, 1), (3, 1), (5, 1), (6, 1), (7, 1)]:
+            do_a(i, first)
 
         wait_all(gv_plane.at[pl.ds(0, 3)], vp_r)
         gv_line[z] = ((gv_plane[0] + gv_plane[1]) + gv_plane[2]) + gv_plane[3]
@@ -173,14 +194,16 @@
 
         def move_mid(j, kind, slot, r):
             at = slot * 2 + kind
-            return remote(mid.at[j, kind], mid_recv.at[slot, kind], m_s, m_r.at[at], dev_z(plane_at(r)))
+            return remote(mid.at[j, kind], mid_recv.at[slot, kind], m_s, pool.at[30 + at], dev_z(plane_at(r)))
 
         def do_mid(j):
             for kind in (1, 0):
                 slot = j * 4 + 3 - kind
                 i = j * 2 + 1 - kind
-                own_copies[slot].wait()
-                pair_copies[slot].wait_recv()
+                if j == 0 and kind == 1:
+                    wait_all(own.at[pl.ds(0, 8)], own_sem.at[2])
+                if j % 2 == 0 and kind == 1:
+                    wait_all(pair.at[pl.ds(0, 4)], pool.at[8 + j // 2])
                 move_a_sum(i, 0).wait_recv()
 
                 def add_a(s, t, kind=kind, slot=slot, i=i):
@@ -226,7 +249,7 @@
             chunks(last, rows, add_mid)
             mid_b_copy.start()
 
-        b_copies = [remote(send_b.at[j], recv_b.at[j], b_s, b_r.at[j], dev_b) for j in range(4)]
+        b_copies = [remote(send_b.at[j], recv_b.at[j], b_s, pool.at[26 + j], dev_b) for j in range(4)]
         z_copies = [remote(send_z.at[j], recv_z.at[z], z_s, z_r, dev_z(order[j])) for j in range(3)]
 
         def do_b(j):
@@ -260,7 +283,6 @@
         vec_end.start()
         do_mid(2)
         merge_mid(0)
-        do_mid(3)
         vec_end.wait_recv()
         gv_sum[pl.ds(pl.multiple_of(core * vstep, 8), vhalf), :] = gv_half[...]
         gv_sum[pl.ds(pl.multiple_of((1 - core) * vstep, 8), vhalf), :] = gv_other[...]
@@ -268,6 +290,7 @@
         do_b(0)
         merge_mid(1)
         do_b(1)
+        do_mid(3)
         do_z(0)
         do_b(2)
         do_z(1)
@@ -277,28 +300,33 @@
         wait_mid(0)
         mid_b_copy.wait_recv()
 
-        def squares(acc, g):
-            return acc + jnp.sum((g * g).reshape(CHUNK // 8, 8, LANES), axis=0)
-
-        def final_mid(i, acc):
-            t = pl.ds(pl.multiple_of(i * CHUNK, 8), CHUNK)
+        def squares(size, total):
+            def add(i, acc):
+                g = total(pl.ds(pl.multiple_of(i * size, 8), size), i)
+                return acc + jnp.sum((g * g).reshape(size // 8, 8, LANES), axis=0)
+
+            return add
+
+        mid_step = (rows - last) // STEPS
+        last_step = last // STEPS
+
+        def final_mid(t, i):
             g = (mid_total(0, t) + mid_b_recv[t, :]) * inv_group
-            grad[pl.ds(pl.multiple_of(last + i * CHUNK, 8), CHUNK), :] = g
-            return squares(acc, g)
-
-        def final_last(i, acc):
-            s = pl.ds(pl.multiple_of(i * CHUNK, 8), CHUNK)
+            grad[pl.ds(pl.multiple_of(last + i * mid_step, 8), mid_step), :] = g
+            return g
+
+        def final_last(s, i):
             g = plane_total(3, s)
             for j in range(3):
                 g = g + recv_z[order[j], s, :]
             g = g * inv_group
             grad[s, :] = g
-            return squares(acc, g)
-
-        sq = lax.fori_loop(0, (rows - last) // CHUNK, final_mid, jnp.zeros((8, LANES), F32))
+            return g
+
+        sq = lax.fori_loop(0, STEPS, squares(mid_step, final_mid), jnp.zeros((8, LANES), F32))
         do_z(3)
         wait_all(recv_z.at[pl.ds(0, 3)], z_r)
-        sq = lax.fori_loop(0, last // CHUNK, final_last, sq)
+        sq = lax.fori_loop(0, STEPS, squares(last_step, final_last), sq)
         norm_rows[me] = jnp.sum(sq, axis=0, keepdims=True)
 
         for d in range(1, group):
@@ -320,123 +348,82 @@
             v_out[s, :] = new_v
             pb_out[me, s, :] = new_p.astype(BF16)
 
-        def move(idx, h, s_sem, r_sem, dev):
-            ref = pb_out.at[idx, halves[h]]
+        def move(idx, p, s_sem, r_sem, dev):
+            ref = pb_out.at[idx, parts[p]]
             return remote(ref, ref, s_sem, r_sem, dev)
 
-        def send_line(r, h, to):
+        def move_line(r, p, kind, to):
             zq = plane_at(r)
-            move(piece(zq, False, False), h, gz_s, gz_r.at[zq * 2 + h], dev_z(plane_at(to))).start()
-
-        def move_b(zq, flip, h):
-            return move(piece(zq, False, flip), h, gb_s, gb_r.at[zq * 2 + h], dev_b)
-
-        def move_a(zq, flip_a, fb, h):
-            i = (zq * 2 + fb) * 2 + h
-            return move(piece(zq, flip_a, fb == 1), h, ga_s, ga_r.at[i], dev_a)
-
-        def move_c(zq, fa, fb, h):
-            return move(piece(zq, fa == 1, fb == 1), h, gc_s, gc_r, dev_c)
-
-        def from_line(r, h, onward_to=None):
+            return move(piece(zq, False, kind == 1), p, gz_s.at[kind], pool.at[zq * 4 + p + kind], dev_z(plane_at(to)))
+
+        def move_b(zq, flip, p):
+            return move(piece(zq, False, flip), p, gb_s.at[p // 2], pool.at[24 if p == 2 else 16 + zq * 2 + p], dev_b)
+
+        def move_a(zq, kind, p):
+            return move(piece(zq, False, kind == 1), p, ga_s, pool.at[25 + zq * 2 + kind], dev_a)
+
+        def move_c(zq, kind, p):
+            return move(piece(zq, False, kind == 1), p, gc_s, gc_r, dev_c)
+
+        def pass_on(r, kind, p):
             zq = plane_at(r)
-            move(piece(zq, False, False), h, gz_s, gz_r.at[zq * 2 + h], dev_z(zq)).wait_recv()
-            if onward_to is not None:
-                send_line(r, h, onward_to)
-            share(r, h)
-
-        def share(r, h):
-            zq = plane_at(r)
-            move_b(zq, False, h).start()
-            move_a(zq, False, 0, h).start()
-            move_c(zq, 0, 0, h).start()
-
-        def from_b(r, h):
-            zq = plane_at(r)
-            move_b(zq, True, h).wait_recv()
-            move_a(zq, False, 1, h).start()
-            move_c(zq, 0, 1, h).start()
-
-        def from_a(r, fb, h):
-            zq = plane_at(r)
-            move_a(zq, True, fb, h).wait_recv()
-            move_c(zq, 1, fb, h).start()
-
-        def finish(line_pieces):
-            wait_all(pb_out.at[pl.ds(0, group // 2)], gc_r)
-            wait_all(pb_out.at[pl.ds(0, line_pieces)], gz_s)
-
-        def update_vector():
+            move_a(zq, kind, p).start()
+            move_c(zq, kind, p).start()
+
+        def gather(own_place, to, plan):
+            def from_line(r, p, kind=0):
+                move_line(r, p, kind, r).wait_recv()
+                if own_place == 1 and r > 1:
+                    move_line(r, p, kind, 0).start()
+                if p < 2:
+                    move_b(plane_at(r), False, p).start()
+                pass_on(r, kind, p)
+
+            def from_b(r, p):
+                move_b(plane_at(r), True, p).wait_recv()
+                if p == 2:
+                    for other in to:
+                        move_line(r, p, 1, other).start()
+                pass_on(r, 1, p)
+
+            def from_a(r, kind):
+                zq = plane_at(r)
+                ref = pb_out.at[piece(zq, True, kind == 1)]
+                wait_all(ref, pool.at[25 + zq * 2 + kind])
+                remote(ref, ref, gc_s, gc_r, dev_c).start()
+
+            for p in range(3):
+                for start, size in steps[p]:
+                    adam(start, size)
+                for other in to:
+                    move_line(own_place, p, 0, other).start()
+                move_b(plane_at(own_place), False, p).start()
+                pass_on(own_place, 0, p)
             pv_new, mv_new, vv_new = adam_update(gv_sum[...] * scale, vec_state[0], vec_state[1], vec_state[2], lr, 0.0)
             pv_out[...] = pv_new
             mv_out[...] = mv_new
             vv_out[...] = vv_new
+            takers = {"z": from_line, "b": from_b, "a": from_a}
+            for item in plan:
+                takers[item[0]](*[int(digit) for digit in item[1:]])
+            wait_all(pb_out.at[pl.ds(0, group // 2)], gc_r)
+            lines = 2 + 2 * own_place
+            wait_all(pb_out.at[pl.ds(0, lines)], gz_s.at[0])
+            wait_all(pb_out.at[pl.ds(0, lines), parts[2]], gz_s.at[1])
 
         @pl.when(place == 0)
         def _():
-            for h in range(2):
-                for start, size in steps[h]:
-                    adam(start, size)
-                send_line(0, h, 1)
-                send_line(0, h, 2)
-                share(0, h)
-            update_vector()
-            for h in range(2):
-                from_line(1, h)
-                from_b(0, h)
-            for h in range(2):
-                from_a(0, 0, h)
-            for r in (1, 2):
-                for h in range(2):
-                    from_line(r + 1, h)
-                    from_b(r, h)
-                for h in range(2):
-                    from_a(r - 1, 1, h)
-                    from_a(r, 0, h)
-            for h in range(2):
-                from_b(3, h)
-                from_a(2, 1, h)
-                from_a(3, 0, h)
-            for h in range(2):
-                from_a(3, 1, h)
-            finish(2)
+            gather(0, (1, 2), END_PLAN)
 
         @pl.when(place == 1)
         def _():
-            for h in range(2):
-                for start, size in steps[h]:
-                    adam(start, size)
-                send_line(1, h, 2)
-                send_line(1, h, 0)
-                share(1, h)
-            update_vector()
-            for h in range(2):
-                from_line(2, h, 0)
-                from_line(0, h)
-                from_b(1, h)
-            for h in range(2):
-                from_a(1, 0, h)
-            for h in range(2):
-                from_line(3, h, 0)
-                from_b(2, h)
-                from_b(0, h)
-            for h in range(2):
-                from_a(1, 1, h)
-                from_a(2, 0, h)
-                from_a(0, 0, h)
-            for h in range(2):
-                from_b(3, h)
-                from_a(2, 1, h)
-                from_a(0, 1, h)
-                from_a(3, 0, h)
-            for h in range(2):
-                from_a(3, 1, h)
-            finish(4)
+            gather(1, (2, 0), INNER_PLAN)
 
         for ref, sem in ((pair, pair_s), (gv_pair, vc_s), (gv_plane.at[pl.ds(0, 3)], vp_s),
                          (gv_line.at[pl.ds(0, 3)], vz_s), (gv_half, ve_s), (send_a, a_s), (send_b, b_s),
                          (send_z.at[pl.ds(0, 3)], z_s), (mid.at[pl.ds(0, 3)], m_s), (mid_b, mb_s), (norm_rows.at[pl.ds(0, group - 1)], n_s),
-                         (pb_out.at[pl.ds(0, 4)], gb_s), (pb_out.at[pl.ds(0, 8)], ga_s),
+                         (pb_out.at[pl.ds(0, 4), pl.ds(0, late)], gb_s.at[0]),
+                         (pb_out.at[0, parts[2]], gb_s.at[1]), (pb_out.at[pl.ds(0, 8)], ga_s),
                          (pb_out.at[pl.ds(0, group // 2)], gc_s)):
             wait_all(ref, sem)
 
@@ -468,9 +455,9 @@
             *[pltpu.VMEM((vhalf, LANES), F32)] * 2,
             pltpu.VMEM((vrows, LANES), F32),
             pltpu.VMEM((3, vrows, LANES), F32),
-            sems((16,)), sem, sems((16,)), sem, sems((16,)), sem, sems((4,)), sem, sem, sem, sems((8,)), sem, sem, sems((3,)),
-            *[sem] * 8, sem, sem,
-            sem, sems((8,)), sem, sems((8,)), sem, sems((16,)), sem, sem,
+            sems((3,)), sems((38,)), *[sem] * 8, sems((3,)),
+            *[sem] * 10,
+            sems((2,)), sems((2,)), sem, sem, sem,
         ],
         compiler_params=pltpu.CompilerParams(
             collective_id=0, has_side_effects=True, vmem_limit_bytes=32 * 1024 * 1024),

time: 80 us -> 77.2 us (0.965)
  Pallas kernels: 78.5 us -> 75.8 us
    pallas_call x1, Pallas kernels: 75.9 us -> 73.2 us  [local_step(): step_kernel(group, rows, vrows, axis_name)(*operands, learn_rate.reshape(1))]
where the time goes in v5:
time: 77.2 us; the launch traced here: 77 us
  Pallas kernels  75.8 us (98%)
  between operations  1.29 us (2%)
    pallas_call x1, Pallas kernels, local_step(): step_kernel(group, rows, vrows, axis_name)(*operands, learn_rate.reshape(1))  73.2 us
    pallas_call x1, Pallas kernels, local_step(): store_kernel([jax.ShapeDtypeStruct(r.shape, r.dtype) for r in results])  2.6 us

profile of v5, /device:TPU:0, one launch (start us, length us, event | category | flops | bytes accessed | tf_op | source)
XLA Modules:
  0.0 77.0 jit_solution(15156563327327079220)
XLA Ops:
  1.3 73.2 %adam_step.1 = (bf16[32,600,128]{2,1,0:T(8,128)(2,1)S(1)}, f32[600,128]{1,0:T(8,128)S(1)}, f32[600,128]{1,0:T(8,128)S(1)}, f32[600,128]{1,0:T(8,128)S(1)}, f32[6...) custom-call(bf16[19200,1,128]{2,1,0:T(2,128)(2,1)} %bitcast.17, bf16[65,1,128]{2,1,0:T(2,128)(2,1)} %bitcast.24, ...), custom_call_target="tpu_custom_call" | custom-call | tf_op jit(solution)/shard_map/adam_step/pallas_call | solution.py:500
  74.4 2.6 %store_results.1 = (bf16[32,600,128]{2,1,0:T(8,128)(2,1)}, f32[600,128]{1,0:T(8,128)}, f32[600,128]{1,0:T(8,128)}, f32[600,128]{1,0:T(8,128)}, f32[65,128]{1,0:T...) custom-call(bf16[32,600,128]{2,1,0:T(8,128)(2,1)S(1)} %get-tuple-element.21.refs_0_, ...), custom_call_target="tpu_custom_call" | custom-call | tf_op jit(solution)/shard_map/store_results/pallas_call | solution.py:501

commit v6 on v5

--- a/solution.py
+++ b/solution.py
@@ -59,8 +59,7 @@
              own, pair, send_a, recv_a, send_b, recv_b, send_z, recv_z, mid, mid_recv, mid_b, mid_b_recv, grad, norm_rows,
              state, gv_own, gv_pair, gv_plane, gv_line, gv_half, gv_other, gv_sum, vec_state,
              own_sem, pool, pair_s, a_s, b_s, z_s, z_r, m_s, mb_s, mb_r, load_sem,
-             vc_s, vc_r, vp_s, vp_r, vz_s, vz_r, ve_s, ve_r, n_s, n_r,
-             gz_s, gb_s, ga_s, gc_s, gc_r):
+             vc_s, vc_r, vp_s, vp_r, vz_s, vz_r, ve_s, ve_r, n_s, n_r):
         me = lax.axis_index(axis_name)
         core = me % 2
         x = (me // 2) % 2
@@ -131,10 +130,17 @@
                 arrival = pool.at[j * 2 + k if k < 2 else 8 + j // 2]
                 pair_copies.append(remote(src, pair.at[j * 4 + k], pair_s, arrival, dev_c))
         vec_pair = remote(gv_ref.at[pl.ds((1 - core) * vstep, vhalf)], gv_pair, vc_s, vc_r, dev_c)
+        src = g_ref.at[pl.ds(partner_piece(order[0], True, True) * rows + last, rows - last)]
+        pair_head = remote(src, pair.at[0, pl.ds(last, rows - last)], pair_s, pool.at[0], dev_c)
+        src = g_ref.at[pl.ds(partner_piece(order[0], True, True) * rows, last)]
+        pair_rest = remote(src, pair.at[0, pl.ds(0, last)], pair_s, pool.at[38], dev_c)
+        pair_head.start()
         for n, i in enumerate(use_order):
-            pair_copies[i].start()
+            if i > 0:
+                pair_copies[i].start()
             if n == 1:
                 vec_pair.start()
+                pair_rest.start()
             if n >= 4:
                 own_copies[i].start()
         for i, ref in enumerate((p_ref, m_ref, v_ref)):
@@ -161,18 +167,25 @@
         def do_a(i, first):
             slot = (i // 2) * 4 + i % 2
             if slot not in loaded:
-                loaded.add(slot)
-                if len(loaded) == 1:
-                    own_copies[0].wait()
+                take(slot)
+            if slot == 0 and first:
+                pair_rest.wait_recv()
+
+            def add_pair(s, _):
+                send_a[i, s, :] = pair_sum(slot, s)
+
+            chunks(*((0, last) if first else (last, rows)), add_pair)
+            move_a_sum(i, first).start()
+
+        def take(slot):
+            loaded.add(slot)
+            if slot == 0:
+                own_copies[0].wait()
+                pair_head.wait_recv()
+            else:
                 if len(loaded) == 2:
                     wait_all(own.at[pl.ds(0, 7)], own_sem.at[1])
                 pair_copies[slot].wait_recv()
-
-            def add_pair(s, _):
-                send_a[i, s, :] = pair_sum(slot, s)
-
-            chunks(*((0, last) if first else (last, rows)), add_pair)
-            move_a_sum(i, first).start()
 
         do_a(0, 0)
 
@@ -297,9 +310,6 @@
         do_z(2)
         do_b(3)
         mid_second()
-        wait_mid(0)
-        mid_b_copy.wait_recv()
-
         def squares(size, total):
             def add(i, acc):
                 g = total(pl.ds(pl.multiple_of(i * size, 8), size), i)
@@ -315,16 +325,22 @@
             grad[pl.ds(pl.multiple_of(last + i * mid_step, 8), mid_step), :] = g
             return g
 
+        def last_plane(s, _):
+            send_z[3, s, :] = plane_total(3, s)
+
         def final_last(s, i):
-            g = plane_total(3, s)
+            g = send_z[3, s, :]
             for j in range(3):
                 g = g + recv_z[order[j], s, :]
             g = g * inv_group
             grad[s, :] = g
             return g
 
+        do_z(3)
+        chunks(0, last, last_plane)
+        wait_mid(0)
+        mid_b_copy.wait_recv()
         sq = lax.fori_loop(0, STEPS, squares(mid_step, final_mid), jnp.zeros((8, LANES), F32))
-        do_z(3)
         wait_all(recv_z.at[pl.ds(0, 3)], z_r)
         sq = lax.fori_loop(0, STEPS, squares(last_step, final_last), sq)
         norm_rows[me] = jnp.sum(sq, axis=0, keepdims=True)
@@ -334,6 +350,11 @@
             remote(norm_rows.at[me], norm_rows.at[me], n_s, n_r, to).start()
         wait_all(state, load_sem.at[1])
         wait_all(vec_state, load_sem.at[2])
+        for ref, sem in ((pair, pair_s), (gv_pair, vc_s), (gv_plane.at[pl.ds(0, 3)], vp_s),
+                         (gv_line.at[pl.ds(0, 3)], vz_s), (gv_half, ve_s), (send_a, a_s), (send_b, b_s),
+                         (send_z.at[pl.ds(0, 3)], z_s), (mid.at[pl.ds(0, 3)], m_s), (mid_b, mb_s),
+                         (norm_rows.at[pl.ds(0, group - 1)], n_s)):
+            wait_all(ref, sem)
         wait_all(norm_rows.at[pl.ds(0, group - 1)], n_r)
         norm_sq = jnp.sum(norm_rows[...]) + vec_sq
         norm = jnp.sqrt(jnp.full((8, LANES), norm_sq, F32))
@@ -354,16 +375,16 @@
 
         def move_line(r, p, kind, to):
             zq = plane_at(r)
-            return move(piece(zq, False, kind == 1), p, gz_s.at[kind], pool.at[zq * 4 + p + kind], dev_z(plane_at(to)))
+            return move(piece(zq, False, kind == 1), p, (m_s if kind else z_s), pool.at[zq * 4 + p + kind], dev_z(plane_at(to)))
 
         def move_b(zq, flip, p):
-            return move(piece(zq, False, flip), p, gb_s.at[p // 2], pool.at[24 if p == 2 else 16 + zq * 2 + p], dev_b)
+            return move(piece(zq, False, flip), p, (mb_s if p == 2 else b_s), pool.at[24 if p == 2 else 16 + zq * 2 + p], dev_b)
 
         def move_a(zq, kind, p):
-            return move(piece(zq, False, kind == 1), p, ga_s, pool.at[25 + zq * 2 + kind], dev_a)
+            return move(piece(zq, False, kind == 1), p, a_s, pool.at[25 + zq * 2 + kind], dev_a)
 
         def move_c(zq, kind, p):
-            return move(piece(zq, False, kind == 1), p, gc_s, gc_r, dev_c)
+            return move(piece(zq, False, kind == 1), p, pair_s, z_r, dev_c)
 
         def pass_on(r, kind, p):
             zq = plane_at(r)
@@ -390,7 +411,7 @@
                 zq = plane_at(r)
                 ref = pb_out.at[piece(zq, True, kind == 1)]
                 wait_all(ref, pool.at[25 + zq * 2 + kind])
-                remote(ref, ref, gc_s, gc_r, dev_c).start()
+                remote(ref, ref, pair_s, z_r, dev_c).start()
 
             for p in range(3):
                 for start, size in steps[p]:
@@ -406,10 +427,10 @@
             takers = {"z": from_line, "b": from_b, "a": from_a}
             for item in plan:
                 takers[item[0]](*[int(digit) for digit in item[1:]])
-            wait_all(pb_out.at[pl.ds(0, group // 2)], gc_r)
+            wait_all(pb_out.at[pl.ds(0, group // 2)], z_r)
             lines = 2 + 2 * own_place
-            wait_all(pb_out.at[pl.ds(0, lines)], gz_s.at[0])
-            wait_all(pb_out.at[pl.ds(0, lines), parts[2]], gz_s.at[1])
+            wait_all(pb_out.at[pl.ds(0, lines)], z_s)
+            wait_all(pb_out.at[pl.ds(0, lines), parts[2]], m_s)
 
         @pl.when(place == 0)
         def _():
@@ -419,12 +440,8 @@
         def _():
             gather(1, (2, 0), INNER_PLAN)
 
-        for ref, sem in ((pair, pair_s), (gv_pair, vc_s), (gv_plane.at[pl.ds(0, 3)], vp_s),
-                         (gv_line.at[pl.ds(0, 3)], vz_s), (gv_half, ve_s), (send_a, a_s), (send_b, b_s),
-                         (send_z.at[pl.ds(0, 3)], z_s), (mid.at[pl.ds(0, 3)], m_s), (mid_b, mb_s), (norm_rows.at[pl.ds(0, group - 1)], n_s),
-                         (pb_out.at[pl.ds(0, 4), pl.ds(0, late)], gb_s.at[0]),
-                         (pb_out.at[0, parts[2]], gb_s.at[1]), (pb_out.at[pl.ds(0, 8)], ga_s),
-                         (pb_out.at[pl.ds(0, group // 2)], gc_s)):
+        for ref, sem in ((pb_out.at[pl.ds(0, 4), pl.ds(0, late)], b_s), (pb_out.at[0, parts[2]], mb_s),
+                         (pb_out.at[pl.ds(0, 8)], a_s), (pb_out.at[pl.ds(0, group // 2)], pair_s)):
             wait_all(ref, sem)
 
     vmem = pl.BlockSpec(memory_space=pltpu.VMEM)
@@ -455,9 +472,8 @@
             *[pltpu.VMEM((vhalf, LANES), F32)] * 2,
             pltpu.VMEM((vrows, LANES), F32),
             pltpu.VMEM((3, vrows, LANES), F32),
-            sems((3,)), sems((38,)), *[sem] * 8, sems((3,)),
+            sems((3,)), sems((39,)), *[sem] * 8, sems((3,)),
             *[sem] * 10,
-            sems((2,)), sems((2,)), sem, sem, sem,
         ],
         compiler_params=pltpu.CompilerParams(
             collective_id=0, has_side_effects=True, vmem_limit_bytes=32 * 1024 * 1024),

time: 77.2 us -> 76.8 us (level)
  no operation moved by 1% of the time
where the time goes in v6:
time: 76.8 us; the launch traced here: 76.7 us
  Pallas kernels  75.4 us (98%)
  between operations  1.29 us (2%)
    pallas_call x1, Pallas kernels, local_step(): step_kernel(group, rows, vrows, axis_name)(*operands, learn_rate.reshape(1))  72.8 us
    pallas_call x1, Pallas kernels, local_step(): store_kernel([jax.ShapeDtypeStruct(r.shape, r.dtype) for r in results])  2.6 us

profile of v6, /device:TPU:0, one launch (start us, length us, event | category | flops | bytes accessed | tf_op | source)
XLA Modules:
  0.0 76.7 jit_solution(9469415988018502696)
XLA Ops:
  1.3 72.8 %adam_step.1 = (bf16[32,600,128]{2,1,0:T(8,128)(2,1)S(1)}, f32[600,128]{1,0:T(8,128)S(1)}, f32[600,128]{1,0:T(8,128)S(1)}, f32[600,128]{1,0:T(8,128)S(1)}, f32[6...) custom-call(bf16[19200,1,128]{2,1,0:T(2,128)(2,1)} %bitcast.17, bf16[65,1,128]{2,1,0:T(2,128)(2,1)} %bitcast.24, ...), custom_call_target="tpu_custom_call" | custom-call | tf_op jit(solution)/shard_map/adam_step/pallas_call | solution.py:516
  74.1 2.6 %store_results.1 = (bf16[32,600,128]{2,1,0:T(8,128)(2,1)}, f32[600,128]{1,0:T(8,128)}, f32[600,128]{1,0:T(8,128)}, f32[600,128]{1,0:T(8,128)}, f32[65,128]{1,0:T...) custom-call(bf16[32,600,128]{2,1,0:T(8,128)(2,1)S(1)} %get-tuple-element.21.refs_0_, ...), custom_call_target="tpu_custom_call" | custom-call | tf_op jit(solution)/shard_map/store_results/pallas_call | solution.py:517

commit v7 on v6

--- a/solution.py
+++ b/solution.py
@@ -23,14 +23,14 @@
 
 
 END_PLAN = [
-    "z100", "b00", "z110", "b01", "b02", "z120", "a00", "z200", "b10", "z210", "b11", "z220",
-    "z121", "a01", "a10", "z300", "b20", "z310", "b21", "z320", "z221", "a11", "a20", "z321",
-    "b30", "b31", "a21", "a30", "a31",
+    "b00", "z100", "z110", "b01", "b02", "b10", "z120", "z200", "z210", "a00", "b11", "z220",
+    "z121", "b20", "a01", "a10", "z300", "z310", "b21", "z320", "a11", "z221", "z321", "b30",
+    "b31", "a30", "a21", "a20", "a31",
 ]
 INNER_PLAN = [
-    "z200", "z000", "b10", "z210", "z010", "b11", "b12", "z220", "z020", "a10", "z300", "b20",
-    "b00", "z310", "b21", "b01", "z320", "z221", "z021", "a11", "a20", "a00", "z321", "b30",
-    "b31", "a21", "a01", "a30", "a31",
+    "z200", "z000", "z210", "a10", "b11", "b12", "b10", "z010", "z220", "z020", "z300", "b20",
+    "b00", "b21", "z021", "z310", "b01", "z320", "z221", "a11", "a20", "a00", "z321", "a01",
+    "b30", "b31", "a31", "a30", "a21",
 ]
 
 
@@ -45,8 +45,10 @@
     inv_group = 1.0 / group
     vstep = vrows // 16 * 8
     vhalf = vrows - vstep
-    last = rows * 3 // 5 // (8 * STEPS) * (8 * STEPS)
-    early, late = 176, 352
+    qstep = vhalf // 32 * 8
+    quarter = vhalf - 3 * qstep
+    last = rows * 16 // 25 // (8 * STEPS) * (8 * STEPS)
+    early, late = 192, 352
     bounds = (0, early, late, rows)
     parts = [pl.ds(lo, hi - lo) for lo, hi in zip(bounds, bounds[1:])]
     steps = []
@@ -57,9 +59,9 @@
     def body(g_ref, gv_ref, p_ref, m_ref, v_ref, pv_ref, mv_ref, vv_ref, lr_ref,
              pb_out, p_out, m_out, v_out, pv_out, mv_out, vv_out,
              own, pair, send_a, recv_a, send_b, recv_b, send_z, recv_z, mid, mid_recv, mid_b, mid_b_recv, grad, norm_rows,
-             state, gv_own, gv_pair, gv_plane, gv_line, gv_half, gv_other, gv_sum, vec_state,
+             state, gv_own, gv_pair, gv_sums, gv_quarter, gv_plane, gv_line, gv_half, gv_other, gv_sum, vec_state,
              own_sem, pool, pair_s, a_s, b_s, z_s, z_r, m_s, mb_s, mb_r, load_sem,
-             vc_s, vc_r, vp_s, vp_r, vz_s, vz_r, ve_s, ve_r, n_s, n_r):
+             vc_s, vc_r, vq_s, vq_r, vp_s, vp_r, vz_s, vz_r, ve_s, ve_r, n_s, n_r):
         me = lax.axis_index(axis_name)
         core = me % 2
         x = (me // 2) % 2
@@ -191,19 +193,28 @@
 
         vec_load.wait()
         vec_pair.wait_recv()
-        gv_plane[spot] = gv_own[:, 0, :].astype(F32) + gv_pair[:, 0, :].astype(F32)
-        vec_plane = [remote(gv_plane.at[spot], gv_plane.at[spot], vp_s, vp_r, dev) for dev in plane]
-        for copy in vec_plane:
-            copy.start()
-
-        for i, first in [(1, 0), (2, 0), (3, 0), (4, 0), (5, 0), (0, 1), (2, 1), (6, 0), (7, 0), (1, 1), (4, 1), (3, 1), (5, 1), (6, 1), (7, 1)]:
+        gv_sums[...] = gv_own[:, 0, :].astype(F32) + gv_pair[:, 0, :].astype(F32)
+
+        def quarter_at(zq):
+            return pl.ds(pl.multiple_of(zq * qstep, 8), quarter)
+
+        for zq in order[:3]:
+            remote(gv_sums.at[quarter_at(zq)], gv_quarter.at[z], vq_s, vq_r, dev_z(zq)).start()
+        gv_quarter[z] = gv_sums[quarter_at(z), :]
+
+        def in_order(parts):
+            return ((parts[0] + parts[1]) + parts[2]) + parts[3]
+
+        for i in range(1, 6):
+            do_a(i, 0)
+
+        wait_all(gv_quarter.at[pl.ds(0, 3)], vq_r)
+        gv_plane[spot] = in_order(gv_quarter)
+        for dev in plane:
+            remote(gv_plane.at[spot], gv_plane.at[spot], vp_s, vp_r, dev).start()
+
+        for i, first in [(0, 1), (2, 1), (7, 0), (1, 1), (6, 0), (4, 1), (3, 1), (5, 1), (6, 1), (7, 1)]:
             do_a(i, first)
-
-        wait_all(gv_plane.at[pl.ds(0, 3)], vp_r)
-        gv_line[z] = ((gv_plane[0] + gv_plane[1]) + gv_plane[2]) + gv_plane[3]
-        vec_line = [remote(gv_line.at[z], gv_line.at[z], vz_s, vz_r, dev_z(order[j])) for j in range(3)]
-        for copy in vec_line:
-            copy.start()
 
         def move_mid(j, kind, slot, r):
             at = slot * 2 + kind
@@ -290,26 +301,32 @@
 
         do_mid(0)
         do_mid(1)
-        wait_all(gv_line.at[pl.ds(0, 3)], vz_r)
-        gv_half[...] = (((gv_line[0] + gv_line[1]) + gv_line[2]) + gv_line[3]) * inv_group
-        vec_end = remote(gv_half, gv_other, ve_s, ve_r, dev_c)
-        vec_end.start()
         do_mid(2)
         merge_mid(0)
-        vec_end.wait_recv()
-        gv_sum[pl.ds(pl.multiple_of(core * vstep, 8), vhalf), :] = gv_half[...]
-        gv_sum[pl.ds(pl.multiple_of((1 - core) * vstep, 8), vhalf), :] = gv_other[...]
-        vec_sq = jnp.sum(gv_sum[...] * gv_sum[...])
         do_b(0)
+        wait_all(gv_plane.at[pl.ds(0, 3)], vp_r)
+        gv_line[z] = in_order(gv_plane) * inv_group
+        for zq in order[:3]:
+            remote(gv_line.at[z], gv_line.at[z], vz_s, vz_r, dev_z(zq)).start()
         merge_mid(1)
         do_b(1)
         do_mid(3)
         do_z(0)
         do_b(2)
         do_z(1)
+        wait_all(gv_line.at[pl.ds(0, 3)], vz_r)
+        for zq in range(4):
+            gv_half[pl.ds(zq * qstep, quarter), :] = gv_line[zq]
+        vec_end = remote(gv_half, gv_other, ve_s, ve_r, dev_c)
+        vec_end.start()
+        vec_end.wait_recv()
+        gv_sum[pl.ds(pl.multiple_of(core * vstep, 8), vhalf), :] = gv_half[...]
+        gv_sum[pl.ds(pl.multiple_of((1 - core) * vstep, 8), vhalf), :] = gv_other[...]
+        vec_sq = jnp.sum(gv_sum[...] * gv_sum[...])
+        mid_second()
         do_z(2)
         do_b(3)
-        mid_second()
+
         def squares(size, total):
             def add(i, acc):
                 g = total(pl.ds(pl.multiple_of(i * size, 8), size), i)
@@ -350,7 +367,7 @@
             remote(norm_rows.at[me], norm_rows.at[me], n_s, n_r, to).start()
         wait_all(state, load_sem.at[1])
         wait_all(vec_state, load_sem.at[2])
-        for ref, sem in ((pair, pair_s), (gv_pair, vc_s), (gv_plane.at[pl.ds(0, 3)], vp_s),
+        for ref, sem in ((pair, pair_s), (gv_pair, vc_s), (gv_quarter.at[pl.ds(0, 3)], vq_s), (gv_plane.at[pl.ds(0, 3)], vp_s),
                          (gv_line.at[pl.ds(0, 3)], vz_s), (gv_half, ve_s), (send_a, a_s), (send_b, b_s),
                          (send_z.at[pl.ds(0, 3)], z_s), (mid.at[pl.ds(0, 3)], m_s), (mid_b, mb_s),
                          (norm_rows.at[pl.ds(0, group - 1)], n_s)):
@@ -380,16 +397,17 @@
         def move_b(zq, flip, p):
             return move(piece(zq, False, flip), p, (mb_s if p == 2 else b_s), pool.at[24 if p == 2 else 16 + zq * 2 + p], dev_b)
 
-        def move_a(zq, kind, p):
-            return move(piece(zq, False, kind == 1), p, a_s, pool.at[25 + zq * 2 + kind], dev_a)
+        def move_a(r, kind, p):
+            zq = plane_at(r)
+            arrival = 33 + p if (r, kind) == (3, 1) else 25 + zq * 2 + kind
+            return move(piece(zq, False, kind == 1), p, a_s, pool.at[arrival], dev_a)
 
         def move_c(zq, kind, p):
             return move(piece(zq, False, kind == 1), p, pair_s, z_r, dev_c)
 
         def pass_on(r, kind, p):
-            zq = plane_at(r)
-            move_a(zq, kind, p).start()
-            move_c(zq, kind, p).start()
+            move_a(r, kind, p).start()
+            move_c(plane_at(r), kind, p).start()
 
         def gather(own_place, to, plan):
             def from_line(r, p, kind=0):
@@ -409,7 +427,13 @@
 
             def from_a(r, kind):
                 zq = plane_at(r)
-                ref = pb_out.at[piece(zq, True, kind == 1)]
+                idx = piece(zq, True, kind == 1)
+                if (r, kind) == (3, 1):
+                    for p in (0, 2, 1):
+                        wait_all(pb_out.at[idx, parts[p]], pool.at[33 + p])
+                        move(idx, p, pair_s, z_r, dev_c).start()
+                    return
+                ref = pb_out.at[idx]
                 wait_all(ref, pool.at[25 + zq * 2 + kind])
                 remote(ref, ref, pair_s, z_r, dev_c).start()
 
@@ -468,12 +492,13 @@
             pltpu.VMEM((group, 1, LANES), F32),
             pltpu.VMEM((3, rows, LANES), F32),
             *[pltpu.VMEM((vhalf, 1, LANES), BF16)] * 2,
-            *[pltpu.VMEM((4, vhalf, LANES), F32)] * 2,
+            pltpu.VMEM((vhalf, LANES), F32),
+            *[pltpu.VMEM((4, quarter, LANES), F32)] * 3,
             *[pltpu.VMEM((vhalf, LANES), F32)] * 2,
             pltpu.VMEM((vrows, LANES), F32),
             pltpu.VMEM((3, vrows, LANES), F32),
             sems((3,)), sems((39,)), *[sem] * 8, sems((3,)),
-            *[sem] * 10,
+            *[sem] * 12,
         ],
         compiler_params=pltpu.CompilerParams(
             collective_id=0, has_side_effects=True, vmem_limit_bytes=32 * 1024 * 1024),

time: 76.8 us -> 76.6 us (level)
  no operation moved by 1% of the time
where the time goes in v7:
time: 76.6 us; the launch traced here: 76.4 us
  Pallas kernels  75.1 us (98%)
  between operations  1.29 us (2%)
    pallas_call x1, Pallas kernels, local_step(): step_kernel(group, rows, vrows, axis_name)(*operands, learn_rate.reshape(1))  72.5 us
    pallas_call x1, Pallas kernels, local_step(): store_kernel([jax.ShapeDtypeStruct(r.shape, r.dtype) for r in results])  2.6 us

profile of v7, /device:TPU:0, one launch (start us, length us, event | category | flops | bytes accessed | tf_op | source)
XLA Modules:
  0.0 76.4 jit_solution(6758115958310327164)
XLA Ops:
  1.3 72.5 %adam_step.1 = (bf16[32,600,128]{2,1,0:T(8,128)(2,1)S(1)}, f32[600,128]{1,0:T(8,128)S(1)}, f32[600,128]{1,0:T(8,128)S(1)}, f32[600,128]{1,0:T(8,128)S(1)}, f32[6...) custom-call(bf16[19200,1,128]{2,1,0:T(2,128)(2,1)} %bitcast.17, bf16[65,1,128]{2,1,0:T(2,128)(2,1)} %bitcast.24, ...), custom_call_target="tpu_custom_call" | custom-call | tf_op jit(solution)/shard_map/adam_step/pallas_call | solution.py:541
  73.8 2.6 %store_results.1 = (bf16[32,600,128]{2,1,0:T(8,128)(2,1)}, f32[600,128]{1,0:T(8,128)}, f32[600,128]{1,0:T(8,128)}, f32[600,128]{1,0:T(8,128)}, f32[65,128]{1,0:T...) custom-call(bf16[32,600,128]{2,1,0:T(8,128)(2,1)S(1)} %get-tuple-element.21.refs_0_, ...), custom_call_target="tpu_custom_call" | custom-call | tf_op jit(solution)/shard_map/store_results/pallas_call | solution.py:542

commit v8 on v7

--- a/solution.py
+++ b/solution.py
@@ -19,7 +19,7 @@
 F32 = jnp.float32
 BF16 = jnp.bfloat16
 LANES = 128
-STEPS = 3
+STEPS = 1
 
 
 END_PLAN = [

time: 76.6 us -> 76.4 us (level)
  no operation moved by 1% of the time
where the time goes in v8:
time: 76.4 us; the launch traced here: 76.3 us
  Pallas kernels  75 us (98%)
  between operations  1.29 us (2%)
    pallas_call x1, Pallas kernels, local_step(): step_kernel(group, rows, vrows, axis_name)(*operands, learn_rate.reshape(1))  72.4 us
    pallas_call x1, Pallas kernels, local_step(): store_kernel([jax.ShapeDtypeStruct(r.shape, r.dtype) for r in results])  2.6 us

profile of v8, /device:TPU:0, one launch (start us, length us, event | category | flops | bytes accessed | tf_op | source)
XLA Modules:
  0.0 76.3 jit_solution(14380202664574946591)
XLA Ops:
  1.3 72.4 %adam_step.1 = (bf16[32,600,128]{2,1,0:T(8,128)(2,1)S(1)}, f32[600,128]{1,0:T(8,128)S(1)}, f32[600,128]{1,0:T(8,128)S(1)}, f32[600,128]{1,0:T(8,128)S(1)}, f32[6...) custom-call(bf16[19200,1,128]{2,1,0:T(2,128)(2,1)} %bitcast.17, bf16[65,1,128]{2,1,0:T(2,128)(2,1)} %bitcast.24, ...), custom_call_target="tpu_custom_call" | custom-call | tf_op jit(solution)/shard_map/adam_step/pallas_call | solution.py:541
  73.7 2.6 %store_results.1 = (bf16[32,600,128]{2,1,0:T(8,128)(2,1)}, f32[600,128]{1,0:T(8,128)}, f32[600,128]{1,0:T(8,128)}, f32[600,128]{1,0:T(8,128)}, f32[65,128]{1,0:T...) custom-call(bf16[32,600,128]{2,1,0:T(8,128)(2,1)S(1)} %get-tuple-element.21.refs_0_, ...), custom_call_target="tpu_custom_call" | custom-call | tf_op jit(solution)/shard_map/store_results/pallas_call | solution.py:542

commit v9 on v8

--- a/solution.py
+++ b/solution.py
@@ -47,7 +47,7 @@
     vhalf = vrows - vstep
     qstep = vhalf // 32 * 8
     quarter = vhalf - 3 * qstep
-    last = rows * 16 // 25 // (8 * STEPS) * (8 * STEPS)
+    last = rows * 47 // 75 // (8 * STEPS) * (8 * STEPS)
     early, late = 192, 352
     bounds = (0, early, late, rows)
     parts = [pl.ds(lo, hi - lo) for lo, hi in zip(bounds, bounds[1:])]

time: 76.4 us -> 76.4 us (level)
  no operation moved by 1% of the time
where the time goes in v9:
time: 76.4 us; the launch traced here: 76.3 us
  Pallas kernels  75 us (98%)
  between operations  1.29 us (2%)
    pallas_call x1, Pallas kernels, local_step(): step_kernel(group, rows, vrows, axis_name)(*operands, learn_rate.reshape(1))  72.4 us
    pallas_call x1, Pallas kernels, local_step(): store_kernel([jax.ShapeDtypeStruct(r.shape, r.dtype) for r in results])  2.6 us

profile of v9, /device:TPU:0, one launch (start us, length us, event | category | flops | bytes accessed | tf_op | source)
XLA Modules:
  0.0 76.3 jit_solution(16853082891974492100)
XLA Ops:
  1.3 72.4 %adam_step.1 = (bf16[32,600,128]{2,1,0:T(8,128)(2,1)S(1)}, f32[600,128]{1,0:T(8,128)S(1)}, f32[600,128]{1,0:T(8,128)S(1)}, f32[600,128]{1,0:T(8,128)S(1)}, f32[6...) custom-call(bf16[19200,1,128]{2,1,0:T(2,128)(2,1)} %bitcast.17, bf16[65,1,128]{2,1,0:T(2,128)(2,1)} %bitcast.24, ...), custom_call_target="tpu_custom_call" | custom-call | tf_op jit(solution)/shard_map/adam_step/pallas_call | solution.py:541
  73.7 2.6 %store_results.1 = (bf16[32,600,128]{2,1,0:T(8,128)(2,1)}, f32[600,128]{1,0:T(8,128)}, f32[600,128]{1,0:T(8,128)}, f32[600,128]{1,0:T(8,128)}, f32[65,128]{1,0:T...) custom-call(bf16[32,600,128]{2,1,0:T(8,128)(2,1)S(1)} %get-tuple-element.21.refs_0_, ...), custom_call_target="tpu_custom_call" | custom-call | tf_op jit(solution)/shard_map/store_results/pallas_call | solution.py:542
